TPU v7x, 32 devices: a 4x4x1 block of a 4x4x8 slice. The times are simulated.
32 devices in a mesh: dp: 1 (over z), tp: 4 (over y), wg: 8 (over x, core).
Axes of the slice: x: 4, y: 4, z: 1, core: 2. Of those that a mesh axis runs over, the one named last changes fastest.
The devices are a block of a 4x4x8 slice.
Arguments:
- tokens: bfloat16 [8192, 1024], P(('dp', 'wg'))
- gain_attn: float32 [1024], P('wg')
- gain_mlp: float32 [1024], P('wg')
- w_qkv: bfloat16 [1024, 3, 16, 64], P('wg', None, 'tp')
- w_rel: bfloat16 [1024, 16, 64], P('wg', 'tp')
- w_out: bfloat16 [16, 64, 1024], P('tp', None, 'wg')
- w_up: bfloat16 [1024, 4096], P('wg', 'tp')
- w_down: bfloat16 [4096, 1024], P('tp', 'wg')
- bias_u: float32 [16, 64], P('tp')
- bias_v: float32 [16, 64], P('tp')
- rel_table: bfloat16 [8, 1024], replicated
- k_cache: bfloat16 [8192, 16, 8, 64], P(('dp', 'wg'), 'tp')
- v_cache: bfloat16 [8192, 16, 8, 64], P(('dp', 'wg'), 'tp')
- positions: int32 [8192], P(('dp', 'wg'))
Outputs:
- output 1: bfloat16 [8192, 1024], P(('dp', 'wg'))
- output 2: bfloat16 [8192, 16, 64], P(('dp', 'wg'), 'tp')
- output 3: bfloat16 [8192, 16, 64], P(('dp', 'wg'), 'tp')
All inputs are finite; a program needn't handle non-finite values.
Results may differ from a plain program's by a relative error of at most 0.0131761.
Values are sent between devices in bfloat16 or wider.
A program may use at most 768 MiB of HBM per device.

v0:
```python
import jax
import jax.numpy as jnp
from jax import lax
from jax.sharding import PartitionSpec as P

NORM_EPS = 1e-6


def rms_norm(row_vals, gain_vec):
    vals_f32 = row_vals.astype(jnp.float32)
    mean_sq = jnp.mean(vals_f32 * vals_f32, axis=-1, keepdims=True)
    return (vals_f32 * lax.rsqrt(mean_sq + NORM_EPS) * gain_vec).astype(jnp.bfloat16)


def cache_attention(q_u, q_v, k_new, v_new, k_cache, v_cache, positions, rel_proj):
    cache_len = k_cache.shape[2]
    score_scale = q_u.shape[-1] ** -0.5
    key_steps = jnp.arange(cache_len)
    is_self = (key_steps[None, :] == positions[:, None])[:, None, :]
    is_valid = (key_steps[None, :] <= positions[:, None])[:, None, :]
    content = jnp.einsum("bhe,bhje->bhj", q_u, k_cache, preferred_element_type=jnp.float32)
    self_score = jnp.einsum("bhe,bhe->bh", q_u, k_new, preferred_element_type=jnp.float32)
    content = jnp.where(is_self, self_score[:, :, None], content)
    rel_all = jnp.einsum("bhe,rhe->bhr", q_v, rel_proj, preferred_element_type=jnp.float32)
    rel_index = jnp.clip(positions[:, None] - key_steps[None, :], 0, cache_len - 1)
    rel_scores = jnp.take_along_axis(rel_all, jnp.broadcast_to(rel_index[:, None, :], rel_all.shape), axis=2)
    scores = jnp.where(is_valid, (content + rel_scores) * score_scale, -1e30)
    attn_probs = jax.nn.softmax(scores, axis=-1).astype(jnp.bfloat16)
    zero_probs = jnp.zeros_like(attn_probs)
    self_prob = jnp.sum(jnp.where(is_self, attn_probs, zero_probs), axis=-1, dtype=jnp.float32)
    cache_probs = jnp.where(is_self, zero_probs, attn_probs)
    attn_out = jnp.einsum("bhj,bhje->bhe", cache_probs, v_cache, preferred_element_type=jnp.float32)
    attn_out = attn_out + self_prob[:, :, None] * v_new.astype(jnp.float32)
    return attn_out.astype(jnp.bfloat16)


def solution(mesh):
    tok_axes = ("dp", "wg")
    in_specs = (P(tok_axes, None), P("wg"), P("wg"), P("wg", None, "tp", None), P("wg", "tp", None), P("tp", None, "wg"), P("wg", "tp"), P("tp", "wg"), P("tp", None), P("tp", None), P(None, None), P(tok_axes, "tp", None, None), P(tok_axes, "tp", None, None), P(tok_axes))
    out_specs = (P(tok_axes, None), P(tok_axes, "tp", None), P(tok_axes, "tp", None))

    def device_step(tokens, gain_attn, gain_mlp, w_qkv, w_rel, w_out, w_up, w_down, bias_u, bias_v, rel_table, k_cache, v_cache, positions):
        gain_attn_full = lax.all_gather(gain_attn, "wg", axis=0, tiled=True)
        gain_mlp_full = lax.all_gather(gain_mlp, "wg", axis=0, tiled=True)
        qkv_full = lax.all_gather(w_qkv, "wg", axis=0, tiled=True)
        rel_full = lax.all_gather(w_rel, "wg", axis=0, tiled=True)
        out_full = lax.all_gather(w_out, "wg", axis=2, tiled=True)
        up_full = lax.all_gather(w_up, "wg", axis=0, tiled=True)
        down_full = lax.all_gather(w_down, "wg", axis=1, tiled=True)
        normed = rms_norm(tokens, gain_attn_full)
        qkv_heads = jnp.einsum("td,dshe->tshe", normed, qkv_full, preferred_element_type=jnp.float32).astype(jnp.bfloat16)
        q_heads = qkv_heads[:, 0]
        k_new = qkv_heads[:, 1]
        v_new = qkv_heads[:, 2]
        rel_proj = jnp.einsum("rd,dhe->rhe", rel_table, rel_full, preferred_element_type=jnp.float32).astype(jnp.bfloat16)
        q_u = (q_heads.astype(jnp.float32) + bias_u).astype(jnp.bfloat16)
        q_v = (q_heads.astype(jnp.float32) + bias_v).astype(jnp.bfloat16)
        attn_out = cache_attention(q_u, q_v, k_new, v_new, k_cache, v_cache, positions, rel_proj)
        attn_part = jnp.einsum("the,hed->td", attn_out, out_full, preferred_element_type=jnp.float32).astype(jnp.bfloat16)
        attn_sum = lax.psum(attn_part, "tp")
        resid = tokens.astype(jnp.float32) + attn_sum.astype(jnp.float32)
        normed_mlp = rms_norm(resid, gain_mlp_full)
        hidden = jax.nn.gelu(jnp.dot(normed_mlp, up_full, preferred_element_type=jnp.float32), approximate=True).astype(jnp.bfloat16)
        mlp_part = jnp.dot(hidden, down_full, preferred_element_type=jnp.float32).astype(jnp.bfloat16)
        mlp_sum = lax.psum(mlp_part, "tp")
        layer_out = (resid + mlp_sum.astype(jnp.float32)).astype(jnp.bfloat16)
        return layer_out, k_new, v_new

    return jax.shard_map(device_step, mesh=mesh, in_specs=in_specs, out_specs=out_specs, check_vma=False)
```

profile of v0, /device:TPU:97, one launch (start us, length us, event | category | flops | bytes accessed | tf_op | source)
XLA Modules:
  0.0 552.6 jit_solution(2858667612884070814)
XLA Ops:
  7.2 0.1 all-gather.6.cloned.1.call-start
  7.3 0.7 all-gather.6.cloned.1.call-update
  8.0 0.1 all-reduce.3.cloned.1.call-start
  8.1 0.7 iota_compare_fusion.1
  8.8 0.9 copy.20
  9.6 0.7 fusion.36
  10.3 1.0 copy.21
  11.4 1.0 copy.22
  12.4 1.7 copy.23
  14.1 4.0 reshape.90
  18.1 0.9 copy.18
  19.0 0.9 copy.19
  19.8 19.3 %all-gather = f32[8,1,128]{2,1,0:T(1,128)S(1)} all-gather(f32[1,1,128]{2,1,0:T(1,128)S(1)} %bitcast.41), channel_id=1, replica_groups=mesh['dp'=1,'tp'=4,'wg'=8] {'wg'}, dimensions={0}, use_global_device_ids=true | all-gather | bytes 4608 | tf_op jit(solution)/shard_map/all_gather | solution.py:43
  39.1 22.7 %all_gather.23 = bf16[1024,4,64]{0,2,1:T(8,128)(2,1)S(1)} all-gather(bf16[128,4,64]{0,2,1:T(8,128)(2,1)S(1)} %copy-done.13), channel_id=1, replica_groups=mesh['dp'=1,'tp'=4,'wg'=8] {'wg'}, dimensions={0}, use_global_device_ids=true | all-gather | bytes 589824 | tf_op jit(solution)/shard_map/all_gather | solution.py:46
  61.8 22.9 %all_gather.24 = bf16[4,64,1024]{2,1,0:T(8,128)(2,1)} all-gather(bf16[4,64,128]{2,1,0:T(8,128)(2,1)S(1)} %copy-done.14), channel_id=1, replica_groups=mesh['dp'=1,'tp'=4,'wg'=8] {'wg'}, dimensions={2}, use_global_device_ids=true | all-gather | bytes 589824 | tf_op jit(solution)/shard_map/all_gather | solution.py:47
  84.7 0.5 fusion.2
  85.2 3.3 fusion.16
  88.5 0.2 convert_element_type.61
  88.8 0.9 slice_bitcast_fusion
  89.7 0.4 copy-done.3
  90.1 0.5 convolution_bitcast_fusion
  90.6 241.3 %gather_fusion = f32[32768]{0:T(1024)S(1)} fusion(f32[1024,4,8]{0,2,1:T(8,128)S(1)} %convolution_bitcast_fusion, s32[32768]{0:T(1024)S(1)} %reshape.90), kind=kCustom, calls=%fused_computation | custom fusion | bytes 655360 | tf_op jit(solution)/shard_map/jit(take_along_axis)/gather | solution.py:26
  331.9 3.8 reshape.93
  335.8 1.8 multiply_reduce_fusion.3
  337.5 3.5 multiply_reduce_fusion.1
  341.0 1.7 copy.36
  342.8 1.7 copy.29
  344.6 12.9 %select_convert_fusion = (f32[1024,4,8]{2,1,0:T(4,128)}, bf16[1024,4,8]{2,1,0:T(4,128)(2,1)}) fusion(pred[1024,8]{1,0:T(8,128)(4,1)S(1)} %copy-done.11, f32[1024,4,8]{2,1,0:T(4,128)S(1)} %copy-done.5, f32[1024,4,8]{2,1,0:T(4,128)} %copy.36, s32[1024,8]{1,0:T(8,128)S(1)} %copy-done.10, s32[1024,8]{1,0:T(8,128)S(1)} %copy-done.9, f32[1024,4]{1,0:T(8,128)} %copy.29, ...), kind=kOutput, calls=%fused_computation.51 | output fusion | flops 466958 | bytes 565248 | tf_op jit(solution)/shard_map/div | solution.py:28
  357.5 2.6 convert_reduce_fusion
  360.0 0.2 copy.24
  360.2 0.8 copy.44
  361.0 3.5 multiply_reduce_fusion
  364.5 2.1 bitcast_convert_fusion
  366.6 0.1 all-reduce.3.cloned.1.call-update
  366.7 0.1 all-gather.10.cloned.1.call-start
  366.8 0.7 all-gather.10.cloned.1.call-update
  367.5 0.1 all-gather.8.cloned.1.call-start
  367.6 0.6 all-gather.8.cloned.1.call-update
  368.1 0.1 all-reduce.5.cloned.1.call-start
  368.2 23.7 %all-gather.1 = f32[8,1,128]{2,1,0:T(1,128)S(1)} all-gather(f32[1,1,128]{2,1,0:T(1,128)S(1)} %bitcast.42), channel_id=1, replica_groups=mesh['dp'=1,'tp'=4,'wg'=8] {'wg'}, dimensions={0}, use_global_device_ids=true | all-gather | bytes 4608 | tf_op jit(solution)/shard_map/all_gather | solution.py:44
  391.9 35.9 %all-reduce.3.cloned.1.call-done = bf16[1024,1024]{1,0:T(8,128)(2,1)} async-done(((bf16[1024,1024]{1,0:T(8,128)(2,1)}), bf16[1024,1024]{1,0:T(8,128)(2,1)}) %all-reduce.3.cloned.1.call-update) | async-done | bytes 2097168 | tf_op jit(solution)/shard_map/psum | solution.py:60
  427.8 2.3 multiply_reduce_fusion.2
  430.2 23.5 %all-gather.10.cloned.1.call-done = bf16[1024,1024]{1,0:T(8,128)(2,1)} async-done(((bf16[1024,128]{1,0:T(8,128)(2,1)}), bf16[1024,1024]{1,0:T(8,128)(2,1)}) %all-gather.10.cloned.1.call-update) | async-done | bytes 2097168 | tf_op jit(solution)/shard_map/all_gather | solution.py:49
  453.7 24.9 %all-gather.8.cloned.1.call-done = bf16[1024,1024]{1,0:T(8,128)(2,1)} async-done(((bf16[128,1024]{1,0:T(8,128)(2,1)}), bf16[1024,1024]{1,0:T(8,128)(2,1)}) %all-gather.8.cloned.1.call-update) | async-done | bytes 2097168 | tf_op jit(solution)/shard_map/all_gather | solution.py:48
  478.6 8.8 %fusion.27 = bf16[1024,1024]{1,0:T(8,128)(2,1)} fusion(bf16[1024,1024]{1,0:T(8,128)(2,1)} %all-gather.10.cloned.1.call-done, bf16[1024,1024]{1,0:T(8,128)(2,1)} %all-gather.8.cloned.1.call-done, bf16[1024,1024]{1,0:T(8,128)(2,1)} %all-reduce.3.cloned.1.call-done, bf16[1024,1024]{1,0:T(8,128)(2,1)S(1)} %copy-done.2, f32[1024]{0:T(1024)S(1)} %bitcast.39, ...), kind=kOutput, calls=%fused_computation.42 | convolution fusion | flops 4311744512 | bytes 10493952 | tf_op jit(solution)/shard_map/dot_general | solution.py:64
  487.4 0.1 all-reduce.5.cloned.1.call-update
  487.4 53.6 %all-reduce.5.cloned.1.call-done = bf16[1024,1024]{1,0:T(8,128)(2,1)} async-done(((bf16[1024,1024]{1,0:T(8,128)(2,1)}), bf16[1024,1024]{1,0:T(8,128)(2,1)}) %all-reduce.5.cloned.1.call-update) | async-done | bytes 2097168 | tf_op jit(solution)/shard_map/psum | solution.py:65
  541.0 5.0 add_convert_fusion
  (41 shorter events, 0.1 us)
Async XLA Ops:
  7.2 82.9 %copy-start = (bf16[8,1024]{1,0:T(8,128)(2,1)S(1)}, bf16[8,1024]{1,0:T(8,128)(2,1)}, u32[]{:S(2)}) copy-start(bf16[8,1024]{1,0:T(8,128)(2,1)} %param.24) | copy-start | bytes 49156
  7.2 78.0 %all-gather.6.cloned.1.call-start = ((), (), s32[]{:S(2)}) async-start(), calls=%async_computation | async-start | bytes 1769472 | tf_op jit(solution)/shard_map/all_gather | solution.py:45
  8.0 419.8 %all-reduce.3.cloned.1.call-start = ((), (), s32[]{:S(2)}) async-start(), calls=%async_computation.1 | async-start | bytes 4194304 | tf_op jit(solution)/shard_map/psum | solution.py:60
  12.4 7.5 %copy-start.17 = (f32[128]{0:T(128)S(1)}, f32[128]{0:T(128)}, u32[]{:S(2)}) copy-start(f32[128]{0:T(128)} %param.15) | copy-start | bytes 1540
  12.4 26.7 %copy-start.13 = (bf16[128,4,64]{0,2,1:T(8,128)(2,1)S(1)}, bf16[128,4,64]{0,2,1:T(8,128)(2,1)}, u32[]{:S(2)}) copy-start(bf16[128,4,64]{0,2,1:T(8,128)(2,1)} %param.18) | copy-start | bytes 196612
  14.1 47.7 %copy-start.14 = (bf16[4,64,128]{2,1,0:T(8,128)(2,1)S(1)}, bf16[4,64,128]{2,1,0:T(8,128)(2,1)}, u32[]{:S(2)}) copy-start(bf16[4,64,128]{2,1,0:T(8,128)(2,1)} %param.19) | copy-start | bytes 196612
  14.1 70.5 %copy-start.1 = (bf16[1024,1024]{1,0:T(8,128)(2,1)S(1)}, bf16[1024,1024]{1,0:T(8,128)(2,1)}, u32[]{:S(2)}) copy-start(bf16[1024,1024]{1,0:T(8,128)(2,1)} %param.14) | copy-start | bytes 6291460
  88.5 1.6 copy-start.15
  88.7 1.3 copy-start.3
  331.9 3.8 copy-start.4
  331.9 3.8 copy-start.16
  337.5 7.0 %copy-start.10 = (s32[1024,8]{1,0:T(8,128)S(1)}, s32[1024,8]{1,0:T(8,128)}, u32[]{:S(2)}) copy-start(s32[1024,8]{1,0:T(8,128)} %copy.22) | copy-start | bytes 98308
  337.5 7.0 %copy-start.12 = (pred[1024,8]{1,0:T(8,128)(4,1)S(1)}, pred[1024,8]{1,0:T(8,128)(4,1)}, u32[]{:S(2)}) copy-start(pred[1024,8]{1,0:T(8,128)(4,1)} %copy.20) | copy-start | bytes 24580
  341.0 3.5 copy-start.5
  341.0 3.5 copy-start.9
  341.0 3.5 copy-start.11
  357.5 2.7 copy-start.6
  361.0 3.5 copy-start.7
  361.0 3.5 copy-start.8
  366.6 1.6 copy-start.18
  366.6 61.2 %copy-start.2 = (bf16[1024,1024]{1,0:T(8,128)(2,1)S(1)}, bf16[1024,1024]{1,0:T(8,128)(2,1)}, u32[]{:S(2)}) copy-start(bf16[1024,1024]{1,0:T(8,128)(2,1)} %param.14) | copy-start | bytes 6291460
  366.7 87.0 %all-gather.10.cloned.1.call-start = ((), (), s32[]{:S(2)}) async-start(), calls=%async_computation.3 | async-start | bytes 2359296 | tf_op jit(solution)/shard_map/all_gather | solution.py:49
  367.5 111.1 %all-gather.8.cloned.1.call-start = ((), (), s32[]{:S(2)}) async-start(), calls=%async_computation.2 | async-start | bytes 2359296 | tf_op jit(solution)/shard_map/all_gather | solution.py:48
  368.1 172.9 %all-reduce.5.cloned.1.call-start = ((), (), s32[]{:S(2)}) async-start(), calls=%async_computation.4 | async-start | bytes 4194304 | tf_op jit(solution)/shard_map/psum | solution.py:65
Sparse Core Ops, SparseCore 0:
  9.6 26.3 all-gather.5
  366.8 60.9 all-reduce.2
  429.4 24.2 all-gather.9
  455.1 23.3 all-gather.7
  487.6 53.4 all-reduce.4
where the time goes:
time: 553 us
  local copies, waits for them, and re-layouts  261 us (47%)
  waiting for transfers between devices  140 us (25%)
  blocking collectives  88.5 us (16%)
  other arithmetic  33.7 us (6%)
  matrix products  14.7 us (3%)
  between operations  14 us (3%)
    gather x4, local copies, waits for them, and re-layouts, cache_attention(): jnp.take_along_axis(rel_all, jnp.broadcast_to(rel_index[:, None, :], rel_...  251 us
    psum x1, waiting for transfers between devices, device_step(): mlp_sum = lax.psum(mlp_part, 'tp')  53.6 us
    psum x1, waiting for transfers between devices, device_step(): attn_sum = lax.psum(attn_part, 'tp')  35.9 us
    all_gather x1, waiting for transfers between devices, device_step(): up_full = lax.all_gather(w_up, 'wg', axis=0, tiled=True)  24.9 us
    all_gather x1, blocking collectives, device_step(): gain_mlp_full = lax.all_gather(gain_mlp, 'wg', axis=0, tiled=True)  23.7 us
    all_gather x1, waiting for transfers between devices, device_step(): down_full = lax.all_gather(w_down, 'wg', axis=1, tiled=True)  23.5 us
    all_gather x1, blocking collectives, device_step(): out_full = lax.all_gather(w_out, 'wg', axis=2, tiled=True)  22.9 us
    all_gather x1, blocking collectives, device_step(): rel_full = lax.all_gather(w_rel, 'wg', axis=0, tiled=True)  22.7 us
  transfers between devices with their start and end apart: 5, of which 4 were waited for; matrix products, arithmetic and copies ran while one was open for 3% of the time, Pallas kernels for 0%

commit v1 on v0

v1 whole, which is shorter than its diff:
```python
import functools

import jax
import jax.numpy as jnp
from jax import lax
from jax.experimental import pallas as pl
from jax.experimental.pallas import tpu as pltpu
from jax.sharding import PartitionSpec as P

NORM_EPS = 1e-6
CORES = 2
CHUNK = 256
MAX_SENDS = 136
MAX_LOCALS = 24
F32, BF16 = jnp.float32, jnp.bfloat16


def dot_nn(a, b):
    return lax.dot_general(a, b, (((1,), (0,)), ((), ())), preferred_element_type=F32)


def dot_nt(a, b):
    return lax.dot_general(a, b, (((1,), (1,)), ((), ())), preferred_element_type=F32)


def aligned(start, size):
    return pl.ds(pl.multiple_of(start, size), size)


def layer_kernel(n_wg, n_tp, dims, tok_hbm, ga_hbm, gm_hbm, wq_hbm, wr_hbm, wo_hbm, wu_hbm, wd_hbm, bu_ref, bv_ref, rt_ref, kc_hbm, vc_hbm, pos_ref,
                 y_hbm, kn_hbm, vn_hbm,
                 tok, kc, vc, gbuf, wqr, wout, wup, wdn, normed, qkv, rel, relp, rels, obuf, otr, hid, z, ybuf, sends, recvs, locs):
    heads, slots, e_dim = dims
    n_tok, d = tok.shape
    he = heads * e_dim
    f_loc = wu_hbm.shape[1]
    piece = d // n_wg
    n_x = n_wg // CORES
    n_chunk = n_tok // CHUNK
    me = lax.axis_index("wg")
    x, c = me // CORES, lax.rem(me, CORES)
    y = lax.axis_index("tp")

    def at_x(off):
        return lax.rem(x + off + n_x, n_x)

    def wg_of(off, core):
        return at_x(off) * CORES + core

    def at_y(off):
        return lax.rem(y + off + n_tp, n_tp)

    other = 1 - c
    dev = {"x+": {"wg": wg_of(1, c)}, "x-": {"wg": wg_of(-1, c)}, "sib": {"wg": x * CORES + other}, "y+": {"tp": at_y(1)}, "y-": {"tp": at_y(-1)}}

    ids, pending = {}, []

    def sem(name):
        return ids.setdefault(name, len(ids))

    def remote(name, view, to):
        i = sem(name)
        return pltpu.make_async_remote_copy(src_ref=view, dst_ref=view, send_sem=sends.at[i], recv_sem=recvs.at[i], device_id=dev[to], device_id_type=pl.DeviceIdType.MESH)

    def send(name, view, to):
        copy = remote(name, view, to)
        copy.start()
        pending.append(copy)

    def recv(name, view, frm="sib"):
        remote(name, view, frm).wait_recv()

    n_local = [0]

    def local(src, dst):
        copy = pltpu.make_async_copy(src, dst, locs.at[n_local[0]])
        n_local[0] += 1
        copy.start()
        return copy

    def x_own(t, view):
        v = view(at_x(0), c, None)
        send(t + "r", v, "x+")
        send(t + "l", v, "x-")
        send(t + "s0", v, "sib")

    def x_relay(t, view, then=None):
        recv(t + "r", view(at_x(-1), c, None))
        send(t + "r2", view(at_x(-1), c, 0), "x+")
        recv(t + "l", view(at_x(1), c, None))
        send(t + "l2", view(at_x(1), c, 1), "x-")
        send(t + "s1", view(at_x(-1), c, None), "sib")
        send(t + "s2", view(at_x(1), c, None), "sib")

    def x_fin(t, view):
        recv(t + "r2", view(at_x(2), c, 0))
        send(t + "s3", view(at_x(2), c, 0), "sib")
        recv(t + "l2", view(at_x(2), c, 1))
        send(t + "s4", view(at_x(2), c, 1), "sib")

    def x_sib(t, view):
        recv(t + "s0", view(at_x(0), other, None))
        recv(t + "s1", view(at_x(-1), other, None))
        recv(t + "s2", view(at_x(1), other, None))
        recv(t + "s3", view(at_x(2), other, 0))
        recv(t + "s4", view(at_x(2), other, 1))

    def y_own(t, view):
        v = view(at_y(0), None, c)
        send(t + "r", v, "y+")
        send(t + "l", v, "y-")

    def y_relay(t, view, share=False):
        recv(t + "r", view(at_y(-1), None, c))
        send(t + "r2", view(at_y(-1), 0, c), "y+")
        recv(t + "l", view(at_y(1), None, c))
        send(t + "l2", view(at_y(1), 1, c), "y-")
        if share:
            send(t + "s1", view(at_y(-1), None, c), "sib")
            send(t + "s2", view(at_y(1), None, c), "sib")

    def y_fin(t, view, share=False):
        recv(t + "r2", view(at_y(2), 0, c))
        if share:
            send(t + "s3", view(at_y(2), 0, c), "sib")
        recv(t + "l2", view(at_y(2), 1, c))
        if share:
            send(t + "s4", view(at_y(2), 1, c), "sib")

    def y_sib_near(t, view):
        recv(t + "s1", view(at_y(-1), None, other))
        recv(t + "s2", view(at_y(1), None, other))

    def y_sib_far(t, view):
        recv(t + "s3", view(at_y(2), 0, other))
        recv(t + "s4", view(at_y(2), 1, other))

    def rows_of(start, size, half):
        if half is None:
            return aligned(start, size)
        return aligned(start + half * (size // 2), size // 2)

    def gain_view(xi, core, half):
        w = xi * CORES + core
        return gbuf.at[w] if half is None else gbuf.at[w, pl.ds(half, 1)]

    def col_view(ref, row0, n_rows):
        def view(xi, core, half):
            return ref.at[rows_of(row0, n_rows, half), aligned((xi * CORES + core) * piece, piece)]
        return view

    wqr_view = col_view(wqr, 0, wqr.shape[0])
    out_view = col_view(wout, 0, wout.shape[0])

    def outy_view(yi, half, core):
        return wout.at[rows_of(yi * he, he, half), aligned((x * CORES + core) * piece, piece)]

    def dny_view(yi, half, core):
        return wdn.at[rows_of(yi * f_loc, f_loc, half), aligned((x * CORES + core) * piece, piece)]

    def dn_view(off):
        return col_view(wdn, at_y(off) * f_loc, f_loc)

    def up_view(xi, core, half):
        return wup.at[rows_of(at_y(0) * d + (xi * CORES + core) * piece, piece, half)]

    def upy_view(off):
        def view(yi, half, core):
            return wup.at[rows_of(yi * d + (at_x(off) * CORES + core) * piece, piece, half)]
        return view

    def o_view(ch):
        def view(yi, half, core):
            return obuf.at[rows_of(ch * CHUNK, CHUNK, half), aligned(yi * he, he)]
        return view

    own_cols = aligned(me * piece, piece)
    n_qkv = wq_hbm.shape[0]
    l_g = [local(ga_hbm, gbuf.at[me, pl.ds(0, 1)]), local(gm_hbm, gbuf.at[me, pl.ds(1, 1)])]
    l_w = [local(wq_hbm, wqr.at[pl.ds(0, n_qkv), own_cols]), local(wr_hbm, wqr.at[pl.ds(n_qkv, he), own_cols])]
    l_o = local(wo_hbm, wout.at[aligned(y * he, he), own_cols])
    l_t = local(tok_hbm, tok)
    l_d = local(wd_hbm, wdn.at[aligned(y * f_loc, f_loc), own_cols])
    l_u = local(wu_hbm, wup.at[aligned(y * d + me * piece, piece)])
    l_k = local(kc_hbm, kc)
    l_v = local(vc_hbm, vc)

    barrier = pltpu.get_barrier_semaphore()
    for to in dev.values():
        pl.semaphore_signal(barrier, inc=1, device_id=to, device_id_type=pl.DeviceIdType.MESH)
    pl.semaphore_wait(barrier, len(dev))

    for copy in l_g:
        copy.wait()
    x_own("g", gain_view)
    for copy in l_w:
        copy.wait()
    x_own("q", wqr_view)
    l_o.wait()
    y_own("oy", outy_view)
    l_d.wait()
    y_own("dy", dny_view)
    x_relay("g", gain_view)
    y_relay("oy", outy_view)
    x_fin("g", gain_view)
    x_sib("g", gain_view)
    l_t.wait()

    def gain_row(i):
        return jnp.concatenate([gbuf[w, i:i + 1, :] for w in range(n_wg)], axis=1)

    def norm(vals, gain):
        mean_sq = jnp.mean(vals * vals, axis=-1, keepdims=True)
        return (vals * lax.rsqrt(mean_sq + NORM_EPS) * gain).astype(BF16)

    norm_rows = 64

    @pl.loop(0, n_tok // norm_rows)
    def _(i):
        r = aligned(i * norm_rows, norm_rows)
        normed[r, :] = norm(tok[r, :].astype(F32), gain_row(0))

    y_fin("oy", outy_view)
    x_relay("q", wqr_view)
    x_own("o", out_view)
    y_relay("dy", dny_view)
    l_u.wait()
    y_own("u0", upy_view(0))
    x_fin("q", wqr_view)
    x_sib("q", wqr_view)

    n_rel = slots * heads * slots
    row = lax.broadcasted_iota(jnp.int32, (n_rel, slots), 0)
    col = lax.broadcasted_iota(jnp.int32, (n_rel, slots), 1)
    offset = jnp.maximum(row // (heads * slots) - lax.rem(row, slots), 0)
    pick = jnp.where(col == offset, 1.0, 0.0).astype(BF16)
    table = dot_nn(pick, rt_ref[...]).astype(BF16)
    rel_q = dot_nt(table, wqr[n_qkv:n_qkv + he, :]).astype(BF16).astype(F32)
    row = lax.broadcasted_iota(jnp.int32, (n_rel, he), 0)
    col = lax.broadcasted_iota(jnp.int32, (n_rel, he), 1)
    relp[...] = jnp.where(lax.rem(row // slots, heads) == col // e_dim, rel_q, 0.0).astype(BF16)

    eye = lax.broadcasted_iota(jnp.int32, (e_dim, e_dim), 0) == lax.broadcasted_iota(jnp.int32, (e_dim, e_dim), 1)

    def bias_col(ref, h):
        return jnp.sum(jnp.where(eye, ref[h:h + 1, :], 0.0), axis=1, keepdims=True)

    l_k.wait()
    l_v.wait()
    scale = e_dim ** -0.5

    def attend(ch):
        cols = pl.ds(ch * CHUNK, CHUNK)
        pos = pos_ref[:, ch * CHUNK:(ch + 1) * CHUNK]
        chunk = normed[ch * CHUNK:(ch + 1) * CHUNK, :]
        qkv[:, cols] = dot_nt(wqr[0:n_qkv, :], chunk).astype(BF16)
        for h in range(heads):
            q = qkv[h * e_dim:(h + 1) * e_dim, cols].astype(F32)
            rel[h * e_dim:(h + 1) * e_dim, :] = (q + bias_col(bv_ref, h)).astype(BF16)
            otr[h * e_dim:(h + 1) * e_dim, :] = (q + bias_col(bu_ref, h)).astype(BF16).astype(F32)
        rel_all = dot_nn(relp[...], rel[...])
        per_p = heads * slots
        sel = jnp.zeros((per_p, CHUNK), F32)
        for p in range(slots):
            sel = jnp.where(pos == p, rel_all[p * per_p:(p + 1) * per_p, :], sel)
        rels[...] = sel

        @pl.loop(0, heads)
        def _(h):
            r = aligned(h * e_dim, e_dim)
            qu = otr[r, :]
            k_new = qkv[aligned(he + h * e_dim, e_dim), cols].astype(F32)
            v_new = qkv[aligned(2 * he + h * e_dim, e_dim), cols].astype(F32)
            rel_h = rels[aligned(h * slots, slots), :]
            self_s = jnp.sum(qu * k_new, axis=0, keepdims=True)
            scores = []
            for j in range(slots):
                s = jnp.sum(qu * kc[h, j, :, cols].astype(F32), axis=0, keepdims=True)
                s = (jnp.where(pos == j, self_s, s) + rel_h[j:j + 1, :]) * scale
                scores.append(jnp.where(pos >= j, s, -1e30))
            top = functools.reduce(jnp.maximum, scores)
            exps = [jnp.exp(s - top) for s in scores]
            total = functools.reduce(jnp.add, exps)
            self_a = jnp.zeros_like(total)
            out = jnp.zeros((e_dim, CHUNK), F32)
            for j in range(slots):
                a = (exps[j] / total).astype(BF16).astype(F32)
                self_a = jnp.where(pos == j, a, self_a)
                out = out + jnp.where(pos > j, a, 0.0) * vc[h, j, :, cols].astype(F32)
            otr[r, :] = out + self_a * v_new

        obuf[ch * CHUNK:(ch + 1) * CHUNK, aligned(y * he, he)] = otr[...].T.astype(BF16)

    def project(ch):
        r = pl.ds(ch * CHUNK, CHUNK)
        hid[r, :] = tok[r, :].astype(F32) + dot_nn(obuf[r, :], wout[...])
        gain = gain_row(1)

        @pl.loop(0, CHUNK // norm_rows)
        def _(i):
            q = aligned(ch * CHUNK + i * norm_rows, norm_rows)
            normed[q, :] = norm(hid[q, :], gain)

    attend(0)
    y_own("a0", o_view(0))
    x_relay("o", out_view)
    x_own("u", up_view)
    attend(1)
    y_own("a1", o_view(1))
    y_relay("a0", o_view(0))
    y_fin("dy", dny_view)
    attend(2)
    y_own("a2", o_view(2))
    y_relay("a1", o_view(1))
    x_fin("o", out_view)
    attend(3)
    y_own("a3", o_view(3))
    y_relay("a2", o_view(2))
    l_kn = local(qkv.at[pl.ds(he, he)], kn_hbm)
    l_vn = local(qkv.at[pl.ds(2 * he, he)], vn_hbm)
    x_relay("u", up_view)
    x_own("d0", dn_view(0))
    x_own("d1", dn_view(-1))
    x_sib("o", out_view)
    y_fin("a0", o_view(0))
    project(0)
    y_relay("a3", o_view(3))
    y_own("u1", upy_view(-1))
    y_own("u2", upy_view(1))
    y_fin("a1", o_view(1))
    project(1)
    x_fin("u", up_view)
    y_own("u3", upy_view(2))
    y_relay("u0", upy_view(0), True)
    y_fin("a2", o_view(2))
    project(2)
    x_sib("u", up_view)
    y_fin("a3", o_view(3))
    project(3)

    def up(off):
        base = at_y(off) * d

        @pl.loop(0, n_chunk)
        def _(i):
            r = aligned(i * CHUNK, CHUNK)
            acc = dot_nn(normed[r, :], wup[aligned(base, d), :])
            z[r, :] = jax.nn.gelu(acc, approximate=True).astype(BF16)

    def down(off):
        base = at_y(off) * f_loc

        @pl.loop(0, n_chunk)
        def _(i):
            r = aligned(i * CHUNK, CHUNK)
            hid[r, :] += dot_nn(z[r, :], wdn[aligned(base, f_loc), :])

    up(0)
    x_relay("d0", dn_view(0))
    x_own("d2", dn_view(1))
    y_relay("u1", upy_view(-1), True)
    y_fin("u0", upy_view(0), True)
    x_fin("d0", dn_view(0))
    x_relay("d1", dn_view(-1))
    x_own("d3", dn_view(2))
    x_sib("d0", dn_view(0))
    down(0)
    y_relay("u2", upy_view(1), True)
    x_fin("d1", dn_view(-1))
    y_fin("u1", upy_view(-1), True)
    y_relay("u3", upy_view(2), True)
    x_relay("d2", dn_view(1))
    for k, off in enumerate((0, -1, 1, 2)):
        y_sib_near("u%d" % k, upy_view(off))
    up(-1)
    x_sib("d1", dn_view(-1))
    x_fin("d2", dn_view(1))
    y_fin("u2", upy_view(1), True)
    down(-1)
    x_relay("d3", dn_view(2))
    y_fin("u3", upy_view(2), True)
    up(1)
    x_fin("d3", dn_view(2))
    x_sib("d2", dn_view(1))
    down(1)
    for k, off in enumerate((0, -1, 1, 2)):
        y_sib_far("u%d" % k, upy_view(off))
    up(2)
    x_sib("d3", dn_view(2))
    base = at_y(2) * f_loc
    outs = []
    for i in range(n_chunk):
        r = pl.ds(i * CHUNK, CHUNK)
        ybuf[r, :] = (hid[r, :] + dot_nn(z[r, :], wdn[aligned(base, f_loc), :])).astype(BF16)
        outs.append(local(ybuf.at[r], y_hbm.at[r]))
    for copy in pending:
        copy.wait_send()
    for copy in [l_kn, l_vn] + outs:
        copy.wait()


def solution(mesh):
    tok_axes = ("dp", "wg")
    in_specs = (P(tok_axes, None), P("wg"), P("wg"), P("wg", None, "tp", None), P("wg", "tp", None), P("tp", None, "wg"), P("wg", "tp"), P("tp", "wg"), P("tp", None), P("tp", None), P(None, None), P(tok_axes, "tp", None, None), P(tok_axes, "tp", None, None), P(tok_axes))
    out_specs = (P(tok_axes, None), P(tok_axes, "tp", None), P(tok_axes, "tp", None))
    n_wg, n_tp = mesh.shape["wg"], mesh.shape["tp"]

    def device_step(tokens, gain_attn, gain_mlp, w_qkv, w_rel, w_out, w_up, w_down, bias_u, bias_v, rel_table, k_cache, v_cache, positions):
        n_tok, d = tokens.shape
        _, heads, slots, e_dim = k_cache.shape
        he = heads * e_dim
        piece, f_loc = w_up.shape
        w_q = jnp.transpose(w_qkv, (1, 2, 3, 0)).reshape(3 * he, piece)
        w_r = jnp.transpose(w_rel, (1, 2, 0)).reshape(he, piece)
        w_o = w_out.reshape(he, piece)
        k_t = jnp.transpose(k_cache, (1, 2, 3, 0))
        v_t = jnp.transpose(v_cache, (1, 2, 3, 0))
        hbm = pl.BlockSpec(memory_space=pl.ANY)
        vmem = pl.BlockSpec(memory_space=pltpu.VMEM)
        y, k_new, v_new = pl.pallas_call(
            functools.partial(layer_kernel, n_wg, n_tp, (heads, slots, e_dim)),
            out_shape=(jax.ShapeDtypeStruct((n_tok, d), BF16), jax.ShapeDtypeStruct((he, n_tok), BF16), jax.ShapeDtypeStruct((he, n_tok), BF16)),
            in_specs=[hbm] * 8 + [vmem] * 3 + [hbm] * 2 + [vmem],
            out_specs=(hbm, hbm, hbm),
            scratch_shapes=[
                pltpu.VMEM((n_tok, d), BF16),
                pltpu.VMEM(k_t.shape, BF16),
                pltpu.VMEM(v_t.shape, BF16),
                pltpu.VMEM((n_wg, 2, piece), F32),
                pltpu.VMEM((4 * he, d), BF16),
                pltpu.VMEM((n_tp * he, d), BF16),
                pltpu.VMEM((n_tp * d, f_loc), BF16),
                pltpu.VMEM((n_tp * f_loc, d), BF16),
                pltpu.VMEM((n_tok, d), BF16),
                pltpu.VMEM((3 * he, n_tok), BF16),
                pltpu.VMEM((he, CHUNK), BF16),
                pltpu.VMEM((slots * heads * slots, he), BF16),
                pltpu.VMEM((heads * slots, CHUNK), F32),
                pltpu.VMEM((n_tok, n_tp * he), BF16),
                pltpu.VMEM((he, CHUNK), F32),
                pltpu.VMEM((n_tok, d), F32),
                pltpu.VMEM((n_tok, f_loc), BF16),
                pltpu.VMEM((n_tok, d), BF16),
                pltpu.SemaphoreType.DMA((MAX_SENDS,)),
                pltpu.SemaphoreType.DMA((MAX_SENDS,)),
                pltpu.SemaphoreType.DMA((MAX_LOCALS,)),
            ],
            compiler_params=pltpu.CompilerParams(collective_id=0, has_side_effects=True, vmem_limit_bytes=67043328),
            name="decoder_layer",
        )(tokens, gain_attn.reshape(1, piece), gain_mlp.reshape(1, piece), w_q, w_r, w_o, w_up, w_down, bias_u, bias_v, rel_table, k_t, v_t, positions.reshape(1, n_tok))
        k_new = jnp.transpose(k_new.reshape(heads, e_dim, n_tok), (2, 0, 1))
        v_new = jnp.transpose(v_new.reshape(heads, e_dim, n_tok), (2, 0, 1))
        return y, k_new, v_new

    return jax.shard_map(device_step, mesh=mesh, in_specs=in_specs, out_specs=out_specs, check_vma=False)
```

time: 553 us -> 106 us (0.19)
  local copies, waits for them, and re-layouts: 261 us -> 4.76 us
  waiting for transfers between devices: 140 us -> 0 us
  Pallas kernels: 0 us -> 100 us
  blocking collectives: 88.5 us -> 0 us
  other arithmetic: 33.7 us -> 0 us
  matrix products: 14.7 us -> 0 us
  between operations: 14 us -> 0.66 us
    gather x4 -> x0, local copies, waits for them, and re-layouts: 251 us -> none  [cache_attention(): jnp.take_along_axis(rel_all, jnp.broadcast_to(rel_index[:, None, :], rel_...]
    pallas_call x0 -> x1, Pallas kernels: none -> 100 us  [device_step(): pl.pallas_call(functools.partial(layer_kernel, n_wg, n_tp, (heads, slots,...]
    psum x2 -> x0, waiting for transfers between devices: 89.5 us -> none  [the longest x1 53.6 us: device_step(): mlp_sum = lax.psum(mlp_part, 'tp')]
    all_gather x4 -> x0, blocking collectives: 88.5 us -> none  [the longest x1 23.7 us: device_step(): gain_mlp_full = lax.all_gather(gain_mlp, 'wg', axis=0, tiled=True)]
    all_gather x3 -> x0, waiting for transfers between devices: 48.4 us -> none  [the longest x1 24.9 us: device_step(): up_full = lax.all_gather(w_up, 'wg', axis=0, tiled=True)]
    div x1 -> x0, other arithmetic: 12.9 us -> none  [cache_attention(): attn_probs = jax.nn.softmax(scores, axis=-1).astype(jnp.bfloat16)]
    dot_general x3 -> x0, matrix products: 11.4 us -> none  [the longest x1 8.79 us: device_step(): jnp.dot(hidden, down_full, preferred_element_type=jnp.float32)]
  transfers between devices with their start and end apart: 5 -> 0, of which waited for: 4 -> 0; matrix products, arithmetic and copies ran while one was open for 3% -> 0% of each run, Pallas kernels for 0% -> 0%
where the time goes in v1:
time: 106 us; the launch traced here: 105 us
  Pallas kernels  100 us (94%)
  local copies, waits for them, and re-layouts  4.76 us (4%)
    pallas_call x1, Pallas kernels, device_step(): pl.pallas_call(functools.partial(layer_kernel, n_wg, n_tp, (heads, slots,...  100 us
    unnamed x7, local copies, waits for them, and re-layouts  4.76 us

profile of v1, /device:TPU:97, one launch (start us, length us, event | category | flops | bytes accessed | tf_op | source)
XLA Modules:
  0.0 105.4 jit_solution(13947418512551698646)
XLA Ops:
  0.6 100.0 %decoder_layer.1 = (bf16[1024,1024]{1,0:T(8,128)(2,1)}, bf16[256,1024]{1,0:T(8,128)(2,1)}, bf16[256,1024]{1,0:T(8,128)(2,1)}) custom-call(bf16[1024,1024]{1,0:T(8,128)(2,1)} %tok_hbm.1, f32[1,128]{1,0:T(1,128)} %bitcast.26, f32[1,128]{1,0:T(1,128)} %bitcast.27, bf16[768,128]{1,0:T(8,128)(2,1)} %bitcast.22, bf16[256,128]{1,0:T(8,128)(2,1)} %bitcast.23, ...), custom_call_target="tpu_custom_call" | custom-call | tf_op jit(solution)/shard_map/decoder_layer/pallas_call | solution.py:420
  100.6 0.0 copy-start.1
  100.6 0.0 copy-start
  100.7 3.2 %copy.20 = bf16[1024,1024]{1,0:T(8,128)(2,1)} copy(bf16[1024,1024]{1,0:T(8,128)(2,1)} %get-tuple-element.12) | data formatting | bytes 4194304
  103.8 0.0 copy-done.1
  103.8 0.8 copy.21
  104.6 0.0 copy-done
  104.6 0.8 copy.22
Async XLA Ops:
  100.6 3.2 %copy-start.1 = (bf16[256,1024]{1,0:T(8,128)(2,1)S(1)}, bf16[256,1024]{1,0:T(8,128)(2,1)}, u32[]{:S(2)}) copy-start(bf16[256,1024]{1,0:T(8,128)(2,1)} %get-tuple-element.7) | copy-start | bytes 1572868
  100.6 4.0 %copy-start = (bf16[256,1024]{1,0:T(8,128)(2,1)S(1)}, bf16[256,1024]{1,0:T(8,128)(2,1)}, u32[]{:S(2)}) copy-start(bf16[256,1024]{1,0:T(8,128)(2,1)} %get-tuple-element.8) | copy-start | bytes 1572868

commit v2 on v1

v2 whole, which is shorter than its diff:
```python
import functools

import jax
import jax.numpy as jnp
from jax import lax
from jax.experimental import pallas as pl
from jax.experimental.pallas import tpu as pltpu
from jax.sharding import PartitionSpec as P

NORM_EPS = 1e-6
CORES = 2
CHUNK = 256
PAIR = 2 * CHUNK
BLOCKS = 4
PARTS = 4
FAMILY_TENSORS, FAMILY_ARRIVALS = 12, 48
TENSORS, ARRIVALS = 21, 80
MAX_LOCALS = 12
F32, BF16 = jnp.float32, jnp.bfloat16


def dot_nn(a, b):
    return lax.dot_general(a, b, (((1,), (0,)), ((), ())), preferred_element_type=F32)


def dot_nt(a, b):
    return lax.dot_general(a, b, (((1,), (1,)), ((), ())), preferred_element_type=F32)


def aligned(start, size):
    return pl.ds(pl.multiple_of(start, size), size)


def layer_kernel(n_wg, n_tp, dims, tok_hbm, ga_hbm, gm_hbm, wq_hbm, wr_hbm, wo_hbm, wu_hbm, wd_hbm, bu_ref, bv_ref, rt_ref, kc_hbm, vc_hbm, pos_ref,
                 y_hbm, kn_hbm, vn_hbm,
                 tok, kc, vc, gbuf, wqr, wout, wup, wdn, normed, qkv, rel, relp, rels, obuf, otr, hid, z, ybuf, sends, recvs, locs):
    heads, slots, e_dim = dims
    n_tok, d = tok.shape
    he = heads * e_dim
    f_loc = wu_hbm.shape[1]
    piece = d // n_wg
    n_x = n_wg // CORES
    n_chunk = n_tok // CHUNK
    blk = f_loc // BLOCKS
    wide = CORES * piece
    me = lax.axis_index("wg")
    x, c = me // CORES, lax.rem(me, CORES)
    y = lax.axis_index("tp")

    def at_x(off):
        return lax.rem(x + off + 2 * n_x, n_x)

    def wg_of(off, core):
        return at_x(off) * CORES + core

    def at_y(off):
        return lax.rem(y + off + n_tp, n_tp)

    other = 1 - c
    dev = {"x+": {"wg": wg_of(1, c)}, "x-": {"wg": wg_of(-1, c)}, "xx": {"wg": wg_of(2, c)}, "sib": {"wg": x * CORES + other}, "y+": {"tp": at_y(1)}, "y-": {"tp": at_y(-1)}}

    families = {"a": (0, 0, ("r", "l", "f")), "v": (4, 12, ("r", "l", "f", "n", "s")), "d": (8, 32, ("r", "l", "f", "s"))}
    tensors, arrivals = {}, {}

    def sem_ids(t, msg):
        if isinstance(t, tuple):
            tensor, base, msgs = families[t[0]]
            return tensor + t[1], base + t[1] * len(msgs) + msgs.index(msg)
        return FAMILY_TENSORS + tensors.setdefault(t, len(tensors)), FAMILY_ARRIVALS + arrivals.setdefault((t, msg), len(arrivals))

    def remote(t, msg, view, to, dst=None):
        i, k = sem_ids(t, msg)
        return pltpu.make_async_remote_copy(src_ref=view, dst_ref=view if dst is None else dst, send_sem=sends.at[i], recv_sem=recvs.at[k], device_id=dev[to], device_id_type=pl.DeviceIdType.MESH)

    def send(t, msg, view, to, dst=None):
        remote(t, msg, view, to, dst).start()

    def recv(t, msg, view):
        remote(t, msg, view, "sib").wait_recv()

    def sent(t, msg, view):
        remote(t, msg, view, "sib").wait_send()

    n_local = [0]

    def local(src, dst):
        copy = pltpu.make_async_copy(src, dst, locs.at[n_local[0]])
        n_local[0] += 1
        copy.start()
        return copy

    def x_own(t, view):
        v = view(0, c, None)
        send(t, "r", v, "x+", view(0, c, None, 1))
        send(t, "l", v, "x-", view(0, c, None, -1))
        send(t, "s", v, "sib")

    def x_relay(t, view):
        recv(t, "r", view(-1, c, None))
        send(t, "f", view(-1, c, 0), "x+", view(-1, c, 0, 1))
        recv(t, "l", view(1, c, None))
        send(t, "f", view(1, c, 1), "x-", view(1, c, 1, -1))
        send(t, "s", view(-1, c, None), "sib")
        send(t, "s", view(1, c, None), "sib")

    def x_fin(t, view):
        recv(t, "f", view(2, c, None))
        send(t, "s", view(2, c, None), "sib")

    def x_sib(t, view):
        recv(t, "s", view.many(n_x))

    def x_sent(t, view):
        sent(t, "r", view.many(n_x + 3))

    def y_own(t, view):
        v = view(at_y(0), None, c)
        send(t, "r", v, "y+")
        send(t, "l", v, "y-")

    def y_relay(t, view, share=False):
        recv(t, "r", view(at_y(-1), None, c))
        send(t, "f", view(at_y(-1), 0, c), "y+")
        recv(t, "l", view(at_y(1), None, c))
        send(t, "f", view(at_y(1), 1, c), "y-")
        if share:
            send(t, "n", view(at_y(-1), None, c), "sib")
            send(t, "n", view(at_y(1), None, c), "sib")

    def y_fin(t, view, share=False):
        recv(t, "f", view(at_y(2), None, c))
        if share:
            send(t, "s", view(at_y(2), None, c), "sib")

    def y_sib_near(t, view):
        recv(t, "n", view.many(2))

    def y_sib_far(t, view):
        recv(t, "s", view(at_y(2), None, other))

    def y_sent(t, view, share=False):
        sent(t, "r", view.many(6 if share else 3))

    def sized(view, many):
        view.many = many
        return view

    def rows_of(start, size, half):
        if half is None:
            return aligned(start, size)
        return aligned(start + half * (size // 2), size // 2)

    def col_view(ref, row0, n_rows):
        def view(off, core, half, hop=0):
            return ref.at[rows_of(row0, n_rows, half), aligned(wg_of(off, core) * piece, piece)]
        return sized(view, lambda n: ref.at[pl.ds(row0, n_rows), pl.ds(0, n * piece)])

    half_q = wqr.shape[0] // 2
    qa_view = col_view(wqr, 0, half_q)
    qb_view = col_view(wqr, half_q, half_q)
    out_view = col_view(wout, 0, wout.shape[0])

    def outy_view(yi, half, core):
        return wout.at[rows_of(yi * he, he, half), aligned(wg_of(0, core) * piece, piece)]

    sized(outy_view, lambda n: wout.at[pl.ds(0, n * he), pl.ds(0, piece)])

    def dny_view(part):
        rows = f_loc // 2

        def view(yi, half, core):
            return wdn.at[yi, rows_of(part * rows, rows, half), aligned(wg_of(0, core) * piece, piece)]
        return sized(view, lambda n: wdn.at[pl.ds(0, n), pl.ds(part * rows, rows), pl.ds(0, piece)])

    def dn_view(b):
        def view(off, core, half, hop=0):
            return wdn.at[:, rows_of(b * blk, blk, half), aligned(wg_of(off, core) * piece, piece)]
        return sized(view, lambda n: wdn.at[:, aligned(b * blk, blk), pl.ds(0, n * piece)])

    def up_view(off, core, half, hop=0):
        return wup.at[y, (off - hop) % n_x, core, rows_of(0, piece, half)]

    sized(up_view, lambda n: wup.at[y, :, :, :, pl.ds(0, n * f_loc // n_wg)])

    def u0_view(yi, half, core):
        return wup.at[yi, 0, core, rows_of(0, piece, half)]

    sized(u0_view, lambda n: wup.at[pl.ds(0, n // CORES), 0])

    def ub_view(b):
        def view(yi, half, core):
            return wup.at[yi, pl.ds(1, n_x - 1), core, rows_of(0, piece, half), aligned(b * blk, blk)]
        return sized(view, lambda n: wup.at[pl.ds(0, n // CORES), pl.ds(1, n_x - 1), :, :, aligned(b * blk, blk)])

    def o_view(ch):
        def view(yi, half, core):
            return obuf.at[rows_of(ch * CHUNK, CHUNK, half), aligned(yi * he, he)]
        return sized(view, lambda n: obuf.at[aligned(ch * CHUNK, CHUNK), pl.ds(0, n * he)])

    own_cols = aligned(me * piece, piece)
    n_qkv = wq_hbm.shape[0]
    l_g = [local(ga_hbm, gbuf.at[me, pl.ds(0, 1)]), local(gm_hbm, gbuf.at[me, pl.ds(1, 1)])]
    l_w = [local(wq_hbm, wqr.at[pl.ds(0, n_qkv), own_cols]), local(wr_hbm, wqr.at[pl.ds(n_qkv, he), own_cols])]
    l_o = local(wo_hbm, wout.at[aligned(y * he, he), own_cols])
    l_t = local(tok_hbm, tok)
    l_d = local(wd_hbm, wdn.at[y, :, own_cols])
    l_u = local(wu_hbm, wup.at[y, 0, c])
    l_k = local(kc_hbm, kc)
    l_v = local(vc_hbm, vc)

    barrier = pltpu.get_barrier_semaphore()
    for to in dev.values():
        pl.semaphore_signal(barrier, inc=1, device_id=to, device_id_type=pl.DeviceIdType.MESH)
    pl.semaphore_wait(barrier, len(dev))

    for copy in l_g:
        copy.wait()
    for to in ("x+", "x-", "xx"):
        send("g", "f", gbuf.at[me], to)
    send("g", "s", gbuf.at[me], "sib")
    for copy in l_w:
        copy.wait()
    x_own("qa", qa_view)
    x_own("qb", qb_view)
    l_o.wait()
    y_own("oy", outy_view)
    l_d.wait()
    y_own("dya", dny_view(0))
    recv("g", "f", gbuf.at[pl.ds(0, n_x - 1)])
    for k in range(1, n_x):
        send("g", "s", gbuf.at[wg_of(k, c)], "sib")
    y_relay("oy", outy_view)
    y_own("dyb", dny_view(1))
    l_u.wait()
    y_own("u0", u0_view)
    x_relay("qa", qa_view)
    recv("g", "s", gbuf.at[pl.ds(0, n_x)])
    l_t.wait()

    def gain_row(i):
        return jnp.concatenate([gbuf[w, i:i + 1, :] for w in range(n_wg)], axis=1)

    def norm(vals, gain):
        mean_sq = jnp.mean(vals * vals, axis=-1, keepdims=True)
        return (vals * lax.rsqrt(mean_sq + NORM_EPS) * gain).astype(BF16)

    norm_rows = 64

    @pl.loop(0, n_tok // norm_rows)
    def _(i):
        r = aligned(i * norm_rows, norm_rows)
        normed[r, :] = norm(tok[r, :].astype(F32), gain_row(0))

    x_relay("qb", qb_view)
    y_fin("oy", outy_view)
    x_own("o", out_view)
    x_own("u", up_view)
    y_relay("dya", dny_view(0))
    y_relay("dyb", dny_view(1))
    x_fin("qa", qa_view)
    x_fin("qb", qb_view)
    x_sib("qa", qa_view)
    x_sib("qb", qb_view)

    n_rel = slots * heads * slots
    row = lax.broadcasted_iota(jnp.int32, (n_rel, slots), 0)
    col = lax.broadcasted_iota(jnp.int32, (n_rel, slots), 1)
    offset = jnp.maximum(row // (heads * slots) - lax.rem(row, slots), 0)
    pick = jnp.where(col == offset, 1.0, 0.0).astype(BF16)
    table = dot_nn(pick, rt_ref[...]).astype(BF16)
    rel_q = dot_nt(table, wqr[n_qkv:n_qkv + he, :]).astype(BF16).astype(F32)
    row = lax.broadcasted_iota(jnp.int32, (n_rel, he), 0)
    col = lax.broadcasted_iota(jnp.int32, (n_rel, he), 1)
    relp[...] = jnp.where(lax.rem(row // slots, heads) == col // e_dim, rel_q, 0.0).astype(BF16)

    eye = lax.broadcasted_iota(jnp.int32, (e_dim, e_dim), 0) == lax.broadcasted_iota(jnp.int32, (e_dim, e_dim), 1)

    def bias_col(ref, h):
        return jnp.sum(jnp.where(eye, ref[h:h + 1, :], 0.0), axis=1, keepdims=True)

    l_k.wait()
    l_v.wait()
    scale = e_dim ** -0.5

    def attend(ch):
        cols = aligned(ch * CHUNK, CHUNK)
        pos = pos_ref[:, cols]
        chunk = normed[cols, :]
        qkv[:, cols] = dot_nt(wqr[0:n_qkv, :], chunk).astype(BF16)
        for h in range(heads):
            q = qkv[h * e_dim:(h + 1) * e_dim, cols].astype(F32)
            rel[h * e_dim:(h + 1) * e_dim, :] = (q + bias_col(bv_ref, h)).astype(BF16)
            otr[h * e_dim:(h + 1) * e_dim, :] = (q + bias_col(bu_ref, h)).astype(BF16).astype(F32)
        rel_all = dot_nn(relp[...], rel[...])
        per_p = heads * slots
        sel = jnp.zeros((per_p, CHUNK), F32)
        for p in range(slots):
            sel = jnp.where(pos == p, rel_all[p * per_p:(p + 1) * per_p, :], sel)
        rels[...] = sel

        @pl.loop(0, heads)
        def _(h):
            r = aligned(h * e_dim, e_dim)
            qu = otr[r, :]
            k_new = qkv[aligned(he + h * e_dim, e_dim), cols].astype(F32)
            v_new = qkv[aligned(2 * he + h * e_dim, e_dim), cols].astype(F32)
            rel_h = rels[aligned(h * slots, slots), :]
            self_s = jnp.sum(qu * k_new, axis=0, keepdims=True)
            scores = []
            for j in range(slots):
                s = jnp.sum(qu * kc[h, j, :, cols].astype(F32), axis=0, keepdims=True)
                s = (jnp.where(pos == j, self_s, s) + rel_h[j:j + 1, :]) * scale
                scores.append(jnp.where(pos >= j, s, -1e30))
            top = functools.reduce(jnp.maximum, scores)
            exps = [jnp.exp(s - top) for s in scores]
            total = functools.reduce(jnp.add, exps)
            self_a = jnp.zeros_like(total)
            out = jnp.zeros((e_dim, CHUNK), F32)
            for j in range(slots):
                a = (exps[j] / total).astype(BF16).astype(F32)
                self_a = jnp.where(pos == j, a, self_a)
                out = out + jnp.where(pos > j, a, 0.0) * vc[h, j, :, cols].astype(F32)
            otr[r, :] = out + self_a * v_new

        obuf[cols, aligned(y * he, he)] = otr[...].T.astype(BF16)

    def project(pair):
        r = aligned(pair * PAIR, PAIR)
        hid[r, :] = tok[r, :].astype(F32) + dot_nn(obuf[r, :], wout[...])
        gain = gain_row(1)

        @pl.loop(0, PAIR // norm_rows)
        def _(i):
            q = aligned(pair * PAIR + i * norm_rows, norm_rows)
            m = norm(hid[q, :], gain)
            for k in range(n_x):
                normed[q, aligned(lax.rem(k - x + n_x, n_x) * wide, wide)] = m[:, k * wide:(k + 1) * wide]

    def up_rows(r, yi, b):
        cols = aligned(b * blk, blk)
        w = wup[yi, :, :, :, cols].reshape(d, blk)
        z[b, r, aligned(yi * blk, blk)] = jax.nn.gelu(dot_nn(normed[r, :], w), approximate=True).astype(BF16)

    def up_own(pair):
        @pl.loop(0, BLOCKS)
        def _(b):
            up_rows(aligned(pair * PAIR, PAIR), y, b)

    def up_near(b):
        @pl.loop(0, 2)
        def _(i):
            up_rows(slice(None), at_y(2 * i - 1), b)

    def up_far(b):
        up_rows(slice(None), at_y(2), b)

    n_out = 4

    def out_copy(i):
        cols = aligned(i * (d // n_out), d // n_out)
        return pltpu.make_async_copy(ybuf.at[:, cols], y_hbm.at[:, cols], locs.at[MAX_LOCALS + i])

    def down(b, last=False):
        w_rows = aligned(b * blk, blk)

        @pl.loop(0, n_out)
        def _(i):
            cols = aligned(i * (d // n_out), d // n_out)
            total = hid[:, cols] + dot_nn(z[b], wdn[:, w_rows, cols].reshape(n_tp * blk, d // n_out))
            if last:
                ybuf[:, cols] = total.astype(BF16)
                out_copy(i).start()
            else:
                hid[:, cols] = total

    @pl.loop(0, n_chunk)
    def _(ch):
        attend(ch)

        @pl.when(ch < 2)
        def _():
            y_own(("a", ch), o_view(ch))

        @pl.when(ch == 1)
        def _():
            x_relay("o", out_view)

    l_kn = local(qkv.at[pl.ds(he, he)], kn_hbm)
    l_vn = local(qkv.at[pl.ds(2 * he, he)], vn_hbm)
    y_relay(("a", 0), o_view(0))
    y_own(("a", 2), o_view(2))
    x_relay("u", up_view)
    y_fin("dya", dny_view(0))
    y_fin("dyb", dny_view(1))
    x_own(("d", 0), dn_view(0))
    x_own(("d", 1), dn_view(1))
    y_relay(("a", 1), o_view(1))
    y_own(("a", 3), o_view(3))
    x_fin("o", out_view)
    y_relay(("a", 2), o_view(2))
    x_sib("o", out_view)

    @pl.loop(0, n_tok // PAIR)
    def _(p):
        for i in range(2):
            y_fin(("a", 2 * p + i), o_view(2 * p + i))
        project(p)

        @pl.when(p == 0)
        def _():
            x_fin("u", up_view)
            y_relay(("a", 3), o_view(3))
            y_own(("v", 0), ub_view(0))
            y_relay("u0", u0_view, True)
            y_own(("v", 1), ub_view(1))
            x_sib("u", up_view)

        up_own(p)

        @pl.when(p == 0)
        def _():
            x_relay(("d", 0), dn_view(0))
            x_own(("d", 2), dn_view(2))

    y_sib_near("u0", u0_view)
    y_relay(("v", 0), ub_view(0), True)
    y_own(("v", 2), ub_view(2))
    x_relay(("d", 1), dn_view(1))
    x_own(("d", 3), dn_view(3))
    y_fin("u0", u0_view, True)

    @pl.loop(0, BLOCKS)
    def _(b):
        y_sib_near(("v", b), ub_view(b))
        up_near(b)

        @pl.when(b == 0)
        def _():
            y_sib_far("u0", u0_view)

        @pl.when(b > 0)
        def _():
            y_sib_far(("v", b - 1), ub_view(b - 1))
            up_far(b - 1)

        @pl.when(b < BLOCKS - 1)
        def _():
            y_relay(("v", b + 1), ub_view(b + 1), True)

        @pl.when(b == 0)
        def _():
            y_own(("v", 3), ub_view(3))

        x_fin(("d", b), dn_view(b))

        @pl.when((b > 0) & (b < BLOCKS - 1))
        def _():
            x_relay(("d", b + 1), dn_view(b + 1))

        @pl.when(b == BLOCKS - 1)
        def _():
            y_fin(("v", b), ub_view(b), True)

        @pl.when(b > 0)
        def _():
            x_sib(("d", b - 1), dn_view(b - 1))
            down(b - 1)

        @pl.when(b < BLOCKS - 1)
        def _():
            y_fin(("v", b), ub_view(b), True)

    sent("g", "f", gbuf.at[pl.ds(0, 2 * n_x - 1)])
    for t, view in (("qa", qa_view), ("qb", qb_view), ("o", out_view), ("u", up_view)):
        x_sent(t, view)
    for t, view, share in (("oy", outy_view, False), ("dya", dny_view(0), False), ("dyb", dny_view(1), False), ("u0", u0_view, True)):
        y_sent(t, view, share)
    for b in range(BLOCKS):
        y_sent(("a", b), o_view(b))
        y_sent(("v", b), ub_view(b), True)
        x_sent(("d", b), dn_view(b))
    for copy in (l_kn, l_vn):
        copy.wait()
    x_sib(("d", BLOCKS - 1), dn_view(BLOCKS - 1))
    y_sib_far(("v", BLOCKS - 1), ub_view(BLOCKS - 1))
    up_far(BLOCKS - 1)
    down(BLOCKS - 1, True)
    for i in range(n_out):
        out_copy(i).wait()
    assert FAMILY_TENSORS + len(tensors) == TENSORS, len(tensors)
    assert FAMILY_ARRIVALS + len(arrivals) == ARRIVALS, len(arrivals)
    assert n_local[0] == MAX_LOCALS, n_local


def write_kernel(parts, *refs):
    n = (len(refs) - 1) // 3
    sems = refs[-1]
    moves = []
    for src, dst, buf in zip(refs[:n], refs[n:2 * n], refs[2 * n:3 * n]):
        rows = src.shape[0] // parts
        for i in range(parts):
            r = pl.ds(i * rows, rows)
            take = pltpu.make_async_copy(src.at[r], buf.at[r], sems.at[2 * len(moves)])
            take.start()
            moves.append((take, pltpu.make_async_copy(buf.at[r], dst.at[r], sems.at[2 * len(moves) + 1])))
    for take, put in moves:
        take.wait()
        put.start()
    for _, put in moves:
        put.wait()


def solution(mesh):
    tok_axes = ("dp", "wg")
    in_specs = (P(tok_axes, None), P("wg"), P("wg"), P("wg", None, "tp", None), P("wg", "tp", None), P("tp", None, "wg"), P("wg", "tp"), P("tp", "wg"), P("tp", None), P("tp", None), P(None, None), P(tok_axes, "tp", None, None), P(tok_axes, "tp", None, None), P(tok_axes))
    out_specs = (P(tok_axes, None), P(tok_axes, "tp", None), P(tok_axes, "tp", None))
    n_wg, n_tp = mesh.shape["wg"], mesh.shape["tp"]

    def device_step(tokens, gain_attn, gain_mlp, w_qkv, w_rel, w_out, w_up, w_down, bias_u, bias_v, rel_table, k_cache, v_cache, positions):
        n_tok, d = tokens.shape
        _, heads, slots, e_dim = k_cache.shape
        he = heads * e_dim
        piece, f_loc = w_up.shape
        w_q = jnp.transpose(w_qkv, (1, 2, 3, 0)).reshape(3 * he, piece)
        w_r = jnp.transpose(w_rel, (1, 2, 0)).reshape(he, piece)
        w_o = w_out.reshape(he, piece)
        k_t = jnp.transpose(k_cache, (1, 2, 3, 0))
        v_t = jnp.transpose(v_cache, (1, 2, 3, 0))
        hbm = pl.BlockSpec(memory_space=pl.ANY)
        vmem = pl.BlockSpec(memory_space=pltpu.VMEM)
        y, k_new, v_new = pl.pallas_call(
            functools.partial(layer_kernel, n_wg, n_tp, (heads, slots, e_dim)),
            out_shape=(jax.ShapeDtypeStruct((n_tok, d), BF16), jax.ShapeDtypeStruct((he, n_tok), BF16), jax.ShapeDtypeStruct((he, n_tok), BF16)),
            in_specs=[hbm] * 8 + [vmem] * 3 + [hbm] * 2 + [vmem],
            out_specs=(hbm, hbm, hbm),
            scratch_shapes=[
                pltpu.VMEM((n_tok, d), BF16),
                pltpu.VMEM(k_t.shape, BF16),
                pltpu.VMEM(v_t.shape, BF16),
                pltpu.VMEM((n_wg, 2, piece), F32),
                pltpu.VMEM((4 * he, d), BF16),
                pltpu.VMEM((n_tp * he, d), BF16),
                pltpu.VMEM((n_tp, n_wg // CORES, CORES, piece, f_loc), BF16),
                pltpu.VMEM((n_tp, f_loc, d), BF16),
                pltpu.VMEM((n_tok, d), BF16),
                pltpu.VMEM((3 * he, n_tok), BF16),
                pltpu.VMEM((he, CHUNK), BF16),
                pltpu.VMEM((slots * heads * slots, he), BF16),
                pltpu.VMEM((heads * slots, CHUNK), F32),
                pltpu.VMEM((n_tok, n_tp * he), BF16),
                pltpu.VMEM((he, CHUNK), F32),
                pltpu.VMEM((n_tok, d), F32),
                pltpu.VMEM((BLOCKS, n_tok, n_tp * (f_loc // BLOCKS)), BF16),
                pltpu.VMEM((n_tok, d), BF16),
                pltpu.SemaphoreType.DMA((TENSORS,)),
                pltpu.SemaphoreType.DMA((ARRIVALS,)),
                pltpu.SemaphoreType.DMA((MAX_LOCALS + 4,)),
            ],
            compiler_params=pltpu.CompilerParams(collective_id=0, has_side_effects=True, vmem_limit_bytes=67043328),
            name="decoder_layer",
        )(tokens, gain_attn.reshape(1, piece), gain_mlp.reshape(1, piece), w_q, w_r, w_o, w_up, w_down, bias_u, bias_v, rel_table, k_t, v_t, positions.reshape(1, n_tok))
        results = (y, k_new, v_new)
        y, k_new, v_new = pl.pallas_call(
            functools.partial(write_kernel, PARTS),
            out_shape=tuple(jax.ShapeDtypeStruct(r.shape, r.dtype) for r in results),
            in_specs=[hbm] * len(results),
            out_specs=(hbm,) * len(results),
            scratch_shapes=[pltpu.VMEM(r.shape, r.dtype) for r in results] + [pltpu.SemaphoreType.DMA((2 * PARTS * len(results),))],
            name="write_results",
        )(*results)
        k_new = jnp.transpose(k_new.reshape(heads, e_dim, n_tok), (2, 0, 1))
        v_new = jnp.transpose(v_new.reshape(heads, e_dim, n_tok), (2, 0, 1))
        return y, k_new, v_new

    return jax.shard_map(device_step, mesh=mesh, in_specs=in_specs, out_specs=out_specs, check_vma=False)
```

time: 106 us -> 86.1 us (0.81)
  Pallas kernels: 100 us -> 85.3 us
  local copies, waits for them, and re-layouts: 4.76 us -> 0 us
    pallas_call x1, Pallas kernels: 100 us -> 82.4 us  [device_step(): pl.pallas_call(functools.partial(layer_kernel, n_wg, n_tp, (heads, slots,...]
    unnamed x7 -> x0, local copies, waits for them, and re-layouts: 4.76 us -> none
    pallas_call x0 -> x1, Pallas kernels: none -> 2.9 us  [device_step(): pl.pallas_call(functools.partial(write_kernel, PARTS), out_shape=tuple((j...]
where the time goes in v2:
time: 86.1 us; the launch traced here: 85.9 us
  Pallas kernels  85.3 us (99%)
    pallas_call x1, Pallas kernels, device_step(): pl.pallas_call(functools.partial(layer_kernel, n_wg, n_tp, (heads, slots,...  82.4 us
    pallas_call x1, Pallas kernels, device_step(): pl.pallas_call(functools.partial(write_kernel, PARTS), out_shape=tuple((j...  2.9 us

profile of v2, /device:TPU:97, one launch (start us, length us, event | category | flops | bytes accessed | tf_op | source)
XLA Modules:
  0.0 85.9 jit_solution(9904478866577618702)
XLA Ops:
  0.6 82.4 %decoder_layer.1 = (bf16[1024,1024]{1,0:T(8,128)(2,1)}, bf16[256,1024]{1,0:T(8,128)(2,1)}, bf16[256,1024]{1,0:T(8,128)(2,1)}) custom-call(bf16[1024,1024]{1,0:T(8,128)(2,1)} %tok_hbm.1, f32[1,128]{1,0:T(1,128)} %bitcast.24, f32[1,128]{1,0:T(1,128)} %bitcast.25, bf16[768,128]{1,0:T(8,128)(2,1)} %bitcast.20, bf16[256,128]{1,0:T(8,128)(2,1)} %bitcast.21, ...), custom_call_target="tpu_custom_call" | custom-call | tf_op jit(solution)/shard_map/decoder_layer/pallas_call | solution.py:531
  83.0 2.9 %write_results.1 = (bf16[1024,1024]{1,0:T(8,128)(2,1)}, bf16[256,1024]{1,0:T(8,128)(2,1)}, bf16[256,1024]{1,0:T(8,128)(2,1)}) custom-call(bf16[1024,1024]{1,0:T(8,128)(2,1)} %get-tuple-element.9.refs_0_, bf16[256,1024]{1,0:T(8,128)(2,1)} %get-tuple-element.10.refs_1_, bf16[256,1024]{1,0:T(8,128)(2,1)} %get-tuple-element.11.refs_2_), custom_call_target="tpu_custom_call" | custom-call | tf_op jit(solution)/shard_map/write_results/pallas_call | solution.py:563

commit v3 on v2

--- a/solution.py
+++ b/solution.py
@@ -1,4 +1,5 @@
 import functools
+import math
 
 import jax
 import jax.numpy as jnp
@@ -8,6 +9,8 @@
 from jax.sharding import PartitionSpec as P
 
 NORM_EPS = 1e-6
+GELU_A = (2.0 / math.pi) ** 0.5
+GELU_B = 0.044715 * GELU_A
 CORES = 2
 CHUNK = 256
 PAIR = 2 * CHUNK
@@ -15,7 +18,7 @@
 PARTS = 4
 FAMILY_TENSORS, FAMILY_ARRIVALS = 12, 48
 TENSORS, ARRIVALS = 21, 80
-MAX_LOCALS = 12
+MAX_LOCALS = 16
 F32, BF16 = jnp.float32, jnp.bfloat16
 
 
@@ -31,9 +34,9 @@
     return pl.ds(pl.multiple_of(start, size), size)
 
 
-def layer_kernel(n_wg, n_tp, dims, tok_hbm, ga_hbm, gm_hbm, wq_hbm, wr_hbm, wo_hbm, wu_hbm, wd_hbm, bu_ref, bv_ref, rt_ref, kc_hbm, vc_hbm, pos_ref,
+def layer_kernel(n_wg, n_tp, dims, tok_hbm, ga_hbm, gm_hbm, wq_hbm, wr_hbm, wo_hbm, wu_hbm, wd_hbm, bu_hbm, bv_hbm, rt_hbm, kc_hbm, vc_hbm, pos_hbm,
                  y_hbm, kn_hbm, vn_hbm,
-                 tok, kc, vc, gbuf, wqr, wout, wup, wdn, normed, qkv, rel, relp, rels, obuf, otr, hid, z, ybuf, sends, recvs, locs):
+                 bu_ref, bv_ref, rt_ref, pos_ref, tok, kc, vc, gbuf, wqr, wout, wup, wdn, normed, qkv, rel, relp, rels, obuf, otr, hid, z, ybuf, sends, recvs, locs):
     heads, slots, e_dim = dims
     n_tok, d = tok.shape
     he = heads * e_dim
@@ -114,29 +117,29 @@
         sent(t, "r", view.many(n_x + 3))
 
     def y_own(t, view):
-        v = view(at_y(0), None, c)
-        send(t, "r", v, "y+")
-        send(t, "l", v, "y-")
+        v = view(0, None, c)
+        send(t, "r", v, "y+", view(0, None, c, 1))
+        send(t, "l", v, "y-", view(0, None, c, -1))
 
     def y_relay(t, view, share=False):
-        recv(t, "r", view(at_y(-1), None, c))
-        send(t, "f", view(at_y(-1), 0, c), "y+")
-        recv(t, "l", view(at_y(1), None, c))
-        send(t, "f", view(at_y(1), 1, c), "y-")
+        recv(t, "r", view(-1, None, c))
+        send(t, "f", view(-1, 0, c), "y+", view(-1, 0, c, 1))
+        recv(t, "l", view(1, None, c))
+        send(t, "f", view(1, 1, c), "y-", view(1, 1, c, -1))
         if share:
-            send(t, "n", view(at_y(-1), None, c), "sib")
-            send(t, "n", view(at_y(1), None, c), "sib")
+            send(t, "n", view(-1, None, c), "sib")
+            send(t, "n", view(1, None, c), "sib")
 
     def y_fin(t, view, share=False):
-        recv(t, "f", view(at_y(2), None, c))
+        recv(t, "f", view(2, None, c))
         if share:
-            send(t, "s", view(at_y(2), None, c), "sib")
+            send(t, "s", view(2, None, c), "sib")
 
     def y_sib_near(t, view):
         recv(t, "n", view.many(2))
 
     def y_sib_far(t, view):
-        recv(t, "s", view(at_y(2), None, other))
+        recv(t, "s", view(2, None, other))
 
     def y_sent(t, view, share=False):
         sent(t, "r", view.many(6 if share else 3))
@@ -160,16 +163,19 @@
     qb_view = col_view(wqr, half_q, half_q)
     out_view = col_view(wout, 0, wout.shape[0])
 
-    def outy_view(yi, half, core):
-        return wout.at[rows_of(yi * he, he, half), aligned(wg_of(0, core) * piece, piece)]
+    def outy_view(off, half, core, hop=0):
+        return wout.at[rows_of(at_y(off) * he, he, half), aligned(wg_of(0, core) * piece, piece)]
 
     sized(outy_view, lambda n: wout.at[pl.ds(0, n * he), pl.ds(0, piece)])
+
+    def slot(off):
+        return (off + 1) % n_tp
 
     def dny_view(part):
         rows = f_loc // 2
 
-        def view(yi, half, core):
-            return wdn.at[yi, rows_of(part * rows, rows, half), aligned(wg_of(0, core) * piece, piece)]
+        def view(off, half, core, hop=0):
+            return wdn.at[slot(off - hop), rows_of(part * rows, rows, half), aligned(wg_of(0, core) * piece, piece)]
         return sized(view, lambda n: wdn.at[pl.ds(0, n), pl.ds(part * rows, rows), pl.ds(0, piece)])
 
     def dn_view(b):
@@ -182,19 +188,19 @@
 
     sized(up_view, lambda n: wup.at[y, :, :, :, pl.ds(0, n * f_loc // n_wg)])
 
-    def u0_view(yi, half, core):
-        return wup.at[yi, 0, core, rows_of(0, piece, half)]
+    def u0_view(off, half, core, hop=0):
+        return wup.at[at_y(off), 0, core, rows_of(0, piece, half)]
 
     sized(u0_view, lambda n: wup.at[pl.ds(0, n // CORES), 0])
 
     def ub_view(b):
-        def view(yi, half, core):
-            return wup.at[yi, pl.ds(1, n_x - 1), core, rows_of(0, piece, half), aligned(b * blk, blk)]
+        def view(off, half, core, hop=0):
+            return wup.at[at_y(off), pl.ds(1, n_x - 1), core, rows_of(0, piece, half), aligned(b * blk, blk)]
         return sized(view, lambda n: wup.at[pl.ds(0, n // CORES), pl.ds(1, n_x - 1), :, :, aligned(b * blk, blk)])
 
     def o_view(ch):
-        def view(yi, half, core):
-            return obuf.at[rows_of(ch * CHUNK, CHUNK, half), aligned(yi * he, he)]
+        def view(off, half, core, hop=0):
+            return obuf.at[rows_of(ch * CHUNK, CHUNK, half), aligned(at_y(off) * he, he)]
         return sized(view, lambda n: obuf.at[aligned(ch * CHUNK, CHUNK), pl.ds(0, n * he)])
 
     own_cols = aligned(me * piece, piece)
@@ -203,8 +209,9 @@
     l_w = [local(wq_hbm, wqr.at[pl.ds(0, n_qkv), own_cols]), local(wr_hbm, wqr.at[pl.ds(n_qkv, he), own_cols])]
     l_o = local(wo_hbm, wout.at[aligned(y * he, he), own_cols])
     l_t = local(tok_hbm, tok)
-    l_d = local(wd_hbm, wdn.at[y, :, own_cols])
+    l_d = local(wd_hbm, wdn.at[slot(0), :, own_cols])
     l_u = local(wu_hbm, wup.at[y, 0, c])
+    l_s = [local(src, dst) for src, dst in ((bu_hbm, bu_ref), (bv_hbm, bv_ref), (rt_hbm, rt_ref), (pos_hbm, pos_ref))]
     l_k = local(kc_hbm, kc)
     l_v = local(vc_hbm, vc)
 
@@ -255,12 +262,15 @@
     y_fin("oy", outy_view)
     x_own("o", out_view)
     x_own("u", up_view)
+    x_fin("qa", qa_view)
+    x_fin("qb", qb_view)
     y_relay("dya", dny_view(0))
     y_relay("dyb", dny_view(1))
-    x_fin("qa", qa_view)
-    x_fin("qb", qb_view)
     x_sib("qa", qa_view)
     x_sib("qb", qb_view)
+
+    for copy in l_s:
+        copy.wait()
 
     n_rel = slots * heads * slots
     row = lax.broadcasted_iota(jnp.int32, (n_rel, slots), 0)
@@ -336,23 +346,46 @@
             for k in range(n_x):
                 normed[q, aligned(lax.rem(k - x + n_x, n_x) * wide, wide)] = m[:, k * wide:(k + 1) * wide]
 
-    def up_rows(r, yi, b):
+    def gelu(v):
+        half = 0.5 * v
+        return half + half * jnp.tanh(v * (GELU_A + GELU_B * (v * v)))
+
+    def up_rows(r, off, b):
         cols = aligned(b * blk, blk)
-        w = wup[yi, :, :, :, cols].reshape(d, blk)
-        z[b, r, aligned(yi * blk, blk)] = jax.nn.gelu(dot_nn(normed[r, :], w), approximate=True).astype(BF16)
+        w = wup[at_y(off), :, :, :, cols].reshape(d, blk)
+        z[b, r, pl.ds(slot(off) * blk, blk)] = gelu(dot_nn(normed[r, :], w)).astype(BF16)
 
     def up_own(pair):
-        @pl.loop(0, BLOCKS)
-        def _(b):
-            up_rows(aligned(pair * PAIR, PAIR), y, b)
-
-    def up_near(b):
-        @pl.loop(0, 2)
+        @pl.loop(0, BLOCKS // 2)
         def _(i):
-            up_rows(slice(None), at_y(2 * i - 1), b)
-
-    def up_far(b):
-        up_rows(slice(None), at_y(2), b)
+            for k in range(2):
+                up_rows(aligned(pair * PAIR, PAIR), 0, 2 * i + k)
+
+    def up_near(b, between=None):
+        @pl.loop(0, n_tok // PAIR)
+        def _(i):
+            for off in (-1, 1):
+                up_rows(aligned(i * PAIR, PAIR), off, b)
+            if between is not None:
+                pl.when(i == 0)(between)
+
+    def down_rows(r, b, first, count):
+        w = wdn[first:first + count, aligned(b * blk, blk), :].reshape(count * blk, d)
+        hid[r, :] += dot_nn(z[b, r, first * blk:(first + count) * blk], w)
+
+    def down_near(b):
+        @pl.loop(0, n_tok // PAIR)
+        def _(i):
+            down_rows(aligned(i * PAIR, PAIR), b, 0, n_tp - 1)
+
+    def far_down(b, first, between=None):
+        @pl.loop(0, n_tok // PAIR)
+        def _(i):
+            r = aligned(i * PAIR, PAIR)
+            up_rows(r, 2, b)
+            down_rows(r, b, first, n_tp - first)
+            if between is not None:
+                pl.when(i == 0)(between)
 
     n_out = 4
 
@@ -360,18 +393,13 @@
         cols = aligned(i * (d // n_out), d // n_out)
         return pltpu.make_async_copy(ybuf.at[:, cols], y_hbm.at[:, cols], locs.at[MAX_LOCALS + i])
 
-    def down(b, last=False):
-        w_rows = aligned(b * blk, blk)
-
-        @pl.loop(0, n_out)
-        def _(i):
-            cols = aligned(i * (d // n_out), d // n_out)
-            total = hid[:, cols] + dot_nn(z[b], wdn[:, w_rows, cols].reshape(n_tp * blk, d // n_out))
-            if last:
-                ybuf[:, cols] = total.astype(BF16)
-                out_copy(i).start()
-            else:
-                hid[:, cols] = total
+    def last_block(b):
+        up_rows(slice(None), 2, b)
+        for i in range(n_out):
+            cols = pl.ds(i * (d // n_out), d // n_out)
+            w = wdn[:, b * blk:(b + 1) * blk, cols].reshape(n_tp * blk, d // n_out)
+            ybuf[:, cols] = (hid[:, cols] + dot_nn(z[b], w)).astype(BF16)
+            out_copy(i).start()
 
     @pl.loop(0, n_chunk)
     def _(ch):
@@ -381,7 +409,7 @@
         def _():
             y_own(("a", ch), o_view(ch))
 
-        @pl.when(ch == 1)
+        @pl.when(ch == 2)
         def _():
             x_relay("o", out_view)
 
@@ -398,6 +426,7 @@
     y_own(("a", 3), o_view(3))
     x_fin("o", out_view)
     y_relay(("a", 2), o_view(2))
+    y_relay("u0", u0_view, True)
     x_sib("o", out_view)
 
     @pl.loop(0, n_tok // PAIR)
@@ -411,7 +440,6 @@
             x_fin("u", up_view)
             y_relay(("a", 3), o_view(3))
             y_own(("v", 0), ub_view(0))
-            y_relay("u0", u0_view, True)
             y_own(("v", 1), ub_view(1))
             x_sib("u", up_view)
 
@@ -428,47 +456,47 @@
     x_relay(("d", 1), dn_view(1))
     x_own(("d", 3), dn_view(3))
     y_fin("u0", u0_view, True)
-
-    @pl.loop(0, BLOCKS)
+    x_fin(("d", 0), dn_view(0))
+    y_sib_near(("v", 0), ub_view(0))
+    up_near(0)
+    y_relay(("v", 1), ub_view(1), True)
+    y_own(("v", 3), ub_view(3))
+    y_sib_far("u0", u0_view)
+    x_sib(("d", 0), dn_view(0))
+    down_near(0)
+
+    @pl.loop(1, BLOCKS)
     def _(b):
         y_sib_near(("v", b), ub_view(b))
-        up_near(b)
-
-        @pl.when(b == 0)
-        def _():
-            y_sib_far("u0", u0_view)
-
-        @pl.when(b > 0)
-        def _():
-            y_sib_far(("v", b - 1), ub_view(b - 1))
-            up_far(b - 1)
+        up_near(b, lambda: y_fin(("v", b - 1), ub_view(b - 1), True))
+        y_sib_far(("v", b - 1), ub_view(b - 1))
 
         @pl.when(b < BLOCKS - 1)
         def _():
-            y_relay(("v", b + 1), ub_view(b + 1), True)
-
-        @pl.when(b == 0)
-        def _():
-            y_own(("v", 3), ub_view(3))
-
-        x_fin(("d", b), dn_view(b))
-
-        @pl.when((b > 0) & (b < BLOCKS - 1))
-        def _():
             x_relay(("d", b + 1), dn_view(b + 1))
 
-        @pl.when(b == BLOCKS - 1)
-        def _():
-            y_fin(("v", b), ub_view(b), True)
-
-        @pl.when(b > 0)
+        def between():
+            @pl.when(b < BLOCKS - 1)
+            def _():
+                y_relay(("v", b + 1), ub_view(b + 1), True)
+
+            @pl.when(b == BLOCKS - 1)
+            def _():
+                y_fin(("v", b), ub_view(b), True)
+                x_fin(("d", b), dn_view(b))
+
+        @pl.when(b == 1)
+        def _():
+            far_down(0, n_tp - 1, between)
+
+        @pl.when(b > 1)
         def _():
             x_sib(("d", b - 1), dn_view(b - 1))
-            down(b - 1)
+            far_down(b - 1, 0, between)
 
         @pl.when(b < BLOCKS - 1)
         def _():
-            y_fin(("v", b), ub_view(b), True)
+            x_fin(("d", b), dn_view(b))
 
     sent("g", "f", gbuf.at[pl.ds(0, 2 * n_x - 1)])
     for t, view in (("qa", qa_view), ("qb", qb_view), ("o", out_view), ("u", up_view)):
@@ -483,8 +511,7 @@
         copy.wait()
     x_sib(("d", BLOCKS - 1), dn_view(BLOCKS - 1))
     y_sib_far(("v", BLOCKS - 1), ub_view(BLOCKS - 1))
-    up_far(BLOCKS - 1)
-    down(BLOCKS - 1, True)
+    last_block(BLOCKS - 1)
     for i in range(n_out):
         out_copy(i).wait()
     assert FAMILY_TENSORS + len(tensors) == TENSORS, len(tensors)
@@ -527,13 +554,16 @@
         k_t = jnp.transpose(k_cache, (1, 2, 3, 0))
         v_t = jnp.transpose(v_cache, (1, 2, 3, 0))
         hbm = pl.BlockSpec(memory_space=pl.ANY)
-        vmem = pl.BlockSpec(memory_space=pltpu.VMEM)
         y, k_new, v_new = pl.pallas_call(
             functools.partial(layer_kernel, n_wg, n_tp, (heads, slots, e_dim)),
             out_shape=(jax.ShapeDtypeStruct((n_tok, d), BF16), jax.ShapeDtypeStruct((he, n_tok), BF16), jax.ShapeDtypeStruct((he, n_tok), BF16)),
-            in_specs=[hbm] * 8 + [vmem] * 3 + [hbm] * 2 + [vmem],
+            in_specs=[hbm] * 14,
             out_specs=(hbm, hbm, hbm),
             scratch_shapes=[
+                pltpu.VMEM(bias_u.shape, F32),
+                pltpu.VMEM(bias_v.shape, F32),
+                pltpu.VMEM(rel_table.shape, BF16),
+                pltpu.VMEM((1, n_tok), jnp.int32),
                 pltpu.VMEM((n_tok, d), BF16),
                 pltpu.VMEM(k_t.shape, BF16),
                 pltpu.VMEM(v_t.shape, BF16),

time: 86.1 us -> 82.5 us (0.958)
  Pallas kernels: 85.3 us -> 81.8 us
    pallas_call x1, Pallas kernels: 82.4 us -> 78.9 us  [device_step(): pl.pallas_call(functools.partial(layer_kernel, n_wg, n_tp, (heads, slots,...]
where the time goes in v3:
time: 82.5 us; the launch traced here: 82.4 us
  Pallas kernels  81.8 us (99%)
    pallas_call x1, Pallas kernels, device_step(): pl.pallas_call(functools.partial(layer_kernel, n_wg, n_tp, (heads, slots,...  78.9 us
    pallas_call x1, Pallas kernels, device_step(): pl.pallas_call(functools.partial(write_kernel, PARTS), out_shape=tuple((j...  2.9 us

profile of v3, /device:TPU:97, one launch (start us, length us, event | category | flops | bytes accessed | tf_op | source)
XLA Modules:
  0.0 82.4 jit_solution(6641893068926155366)
XLA Ops:
  0.6 78.9 %decoder_layer.1 = (bf16[1024,1024]{1,0:T(8,128)(2,1)}, bf16[256,1024]{1,0:T(8,128)(2,1)}, bf16[256,1024]{1,0:T(8,128)(2,1)}) custom-call(bf16[1024,1024]{1,0:T(8,128)(2,1)} %tok_hbm.1, f32[1,128]{1,0:T(1,128)} %bitcast.24, f32[1,128]{1,0:T(1,128)} %bitcast.25, bf16[768,128]{1,0:T(8,128)(2,1)} %bitcast.20, bf16[256,128]{1,0:T(8,128)(2,1)} %bitcast.21, ...), custom_call_target="tpu_custom_call" | custom-call | tf_op jit(solution)/shard_map/decoder_layer/pallas_call | solution.py:557
  79.5 2.9 %write_results.1 = (bf16[1024,1024]{1,0:T(8,128)(2,1)}, bf16[256,1024]{1,0:T(8,128)(2,1)}, bf16[256,1024]{1,0:T(8,128)(2,1)}) custom-call(bf16[1024,1024]{1,0:T(8,128)(2,1)} %get-tuple-element.9.refs_0_, bf16[256,1024]{1,0:T(8,128)(2,1)} %get-tuple-element.10.refs_1_, bf16[256,1024]{1,0:T(8,128)(2,1)} %get-tuple-element.11.refs_2_), custom_call_target="tpu_custom_call" | custom-call | tf_op jit(solution)/shard_map/write_results/pallas_call | solution.py:593

commit v4 on v3

--- a/solution.py
+++ b/solution.py
@@ -15,10 +15,11 @@
 CHUNK = 256
 PAIR = 2 * CHUNK
 BLOCKS = 4
-PARTS = 4
+PARTS = 2
+KERNEL_VMEM = 55574528
 FAMILY_TENSORS, FAMILY_ARRIVALS = 12, 48
 TENSORS, ARRIVALS = 21, 80
-MAX_LOCALS = 16
+MAX_LOCALS = 14
 F32, BF16 = jnp.float32, jnp.bfloat16
 
 
@@ -35,8 +36,8 @@
 
 
 def layer_kernel(n_wg, n_tp, dims, tok_hbm, ga_hbm, gm_hbm, wq_hbm, wr_hbm, wo_hbm, wu_hbm, wd_hbm, bu_hbm, bv_hbm, rt_hbm, kc_hbm, vc_hbm, pos_hbm,
-                 y_hbm, kn_hbm, vn_hbm,
-                 bu_ref, bv_ref, rt_ref, pos_ref, tok, kc, vc, gbuf, wqr, wout, wup, wdn, normed, qkv, rel, relp, rels, obuf, otr, hid, z, ybuf, sends, recvs, locs):
+                 y_out, kn_out, vn_out,
+                 bu_ref, bv_ref, rt_ref, pos_ref, tok, kc, vc, gbuf, wqr, wout, wup, wdn, normed, qkv, rel, relp, rels, obuf, otr, hid, z, sends, recvs, locs):
     heads, slots, e_dim = dims
     n_tok, d = tok.shape
     he = heads * e_dim
@@ -389,17 +390,12 @@
 
     n_out = 4
 
-    def out_copy(i):
-        cols = aligned(i * (d // n_out), d // n_out)
-        return pltpu.make_async_copy(ybuf.at[:, cols], y_hbm.at[:, cols], locs.at[MAX_LOCALS + i])
-
     def last_block(b):
         up_rows(slice(None), 2, b)
         for i in range(n_out):
             cols = pl.ds(i * (d // n_out), d // n_out)
             w = wdn[:, b * blk:(b + 1) * blk, cols].reshape(n_tp * blk, d // n_out)
-            ybuf[:, cols] = (hid[:, cols] + dot_nn(z[b], w)).astype(BF16)
-            out_copy(i).start()
+            y_out[:, cols] = (hid[:, cols] + dot_nn(z[b], w)).astype(BF16)
 
     @pl.loop(0, n_chunk)
     def _(ch):
@@ -413,8 +409,6 @@
         def _():
             x_relay("o", out_view)
 
-    l_kn = local(qkv.at[pl.ds(he, he)], kn_hbm)
-    l_vn = local(qkv.at[pl.ds(2 * he, he)], vn_hbm)
     y_relay(("a", 0), o_view(0))
     y_own(("a", 2), o_view(2))
     x_relay("u", up_view)
@@ -424,6 +418,8 @@
     x_own(("d", 1), dn_view(1))
     y_relay(("a", 1), o_view(1))
     y_own(("a", 3), o_view(3))
+    kn_out[...] = qkv[he:2 * he, :]
+    vn_out[...] = qkv[2 * he:3 * he, :]
     x_fin("o", out_view)
     y_relay(("a", 2), o_view(2))
     y_relay("u0", u0_view, True)
@@ -507,33 +503,26 @@
         y_sent(("a", b), o_view(b))
         y_sent(("v", b), ub_view(b), True)
         x_sent(("d", b), dn_view(b))
-    for copy in (l_kn, l_vn):
-        copy.wait()
     x_sib(("d", BLOCKS - 1), dn_view(BLOCKS - 1))
     y_sib_far(("v", BLOCKS - 1), ub_view(BLOCKS - 1))
     last_block(BLOCKS - 1)
-    for i in range(n_out):
-        out_copy(i).wait()
     assert FAMILY_TENSORS + len(tensors) == TENSORS, len(tensors)
     assert FAMILY_ARRIVALS + len(arrivals) == ARRIVALS, len(arrivals)
     assert n_local[0] == MAX_LOCALS, n_local
 
 
 def write_kernel(parts, *refs):
-    n = (len(refs) - 1) // 3
+    n = (len(refs) - 1) // 2
     sems = refs[-1]
-    moves = []
-    for src, dst, buf in zip(refs[:n], refs[n:2 * n], refs[2 * n:3 * n]):
+    puts = []
+    for src, dst in zip(refs[:n], refs[n:2 * n]):
         rows = src.shape[0] // parts
         for i in range(parts):
             r = pl.ds(i * rows, rows)
-            take = pltpu.make_async_copy(src.at[r], buf.at[r], sems.at[2 * len(moves)])
-            take.start()
-            moves.append((take, pltpu.make_async_copy(buf.at[r], dst.at[r], sems.at[2 * len(moves) + 1])))
-    for take, put in moves:
-        take.wait()
+            puts.append(pltpu.make_async_copy(src.at[r], dst.at[r], sems.at[len(puts)]))
+    for put in puts:
         put.start()
-    for _, put in moves:
+    for put in puts:
         put.wait()
 
 
@@ -554,11 +543,12 @@
         k_t = jnp.transpose(k_cache, (1, 2, 3, 0))
         v_t = jnp.transpose(v_cache, (1, 2, 3, 0))
         hbm = pl.BlockSpec(memory_space=pl.ANY)
+        vmem = pl.BlockSpec(memory_space=pltpu.VMEM)
         y, k_new, v_new = pl.pallas_call(
             functools.partial(layer_kernel, n_wg, n_tp, (heads, slots, e_dim)),
-            out_shape=(jax.ShapeDtypeStruct((n_tok, d), BF16), jax.ShapeDtypeStruct((he, n_tok), BF16), jax.ShapeDtypeStruct((he, n_tok), BF16)),
+            out_shape=(pltpu.VMEM((n_tok, d), BF16), pltpu.VMEM((he, n_tok), BF16), pltpu.VMEM((he, n_tok), BF16)),
             in_specs=[hbm] * 14,
-            out_specs=(hbm, hbm, hbm),
+            out_specs=(vmem, vmem, vmem),
             scratch_shapes=[
                 pltpu.VMEM(bias_u.shape, F32),
                 pltpu.VMEM(bias_v.shape, F32),
@@ -581,21 +571,21 @@
                 pltpu.VMEM((he, CHUNK), F32),
                 pltpu.VMEM((n_tok, d), F32),
                 pltpu.VMEM((BLOCKS, n_tok, n_tp * (f_loc // BLOCKS)), BF16),
-                pltpu.VMEM((n_tok, d), BF16),
                 pltpu.SemaphoreType.DMA((TENSORS,)),
                 pltpu.SemaphoreType.DMA((ARRIVALS,)),
-                pltpu.SemaphoreType.DMA((MAX_LOCALS + 4,)),
+                pltpu.SemaphoreType.DMA((MAX_LOCALS,)),
             ],
-            compiler_params=pltpu.CompilerParams(collective_id=0, has_side_effects=True, vmem_limit_bytes=67043328),
+            compiler_params=pltpu.CompilerParams(collective_id=0, has_side_effects=True, vmem_limit_bytes=KERNEL_VMEM),
             name="decoder_layer",
         )(tokens, gain_attn.reshape(1, piece), gain_mlp.reshape(1, piece), w_q, w_r, w_o, w_up, w_down, bias_u, bias_v, rel_table, k_t, v_t, positions.reshape(1, n_tok))
         results = (y, k_new, v_new)
         y, k_new, v_new = pl.pallas_call(
             functools.partial(write_kernel, PARTS),
             out_shape=tuple(jax.ShapeDtypeStruct(r.shape, r.dtype) for r in results),
-            in_specs=[hbm] * len(results),
+            in_specs=[vmem] * len(results),
             out_specs=(hbm,) * len(results),
-            scratch_shapes=[pltpu.VMEM(r.shape, r.dtype) for r in results] + [pltpu.SemaphoreType.DMA((2 * PARTS * len(results),))],
+            scratch_shapes=[pltpu.SemaphoreType.DMA((PARTS * len(results),))],
+            compiler_params=pltpu.CompilerParams(vmem_limit_bytes=4 << 20),
             name="write_results",
         )(*results)
         k_new = jnp.transpose(k_new.reshape(heads, e_dim, n_tok), (2, 0, 1))

time: 82.5 us -> 80.2 us (0.972)
  Pallas kernels: 81.8 us -> 79.4 us
    pallas_call x1, Pallas kernels: 2.9 us -> 1.71 us  [device_step(): pl.pallas_call(functools.partial(write_kernel, PARTS), out_shape=tuple((j...]
    pallas_call x1, Pallas kernels: 78.9 us -> 77.7 us  [device_step(): pl.pallas_call(functools.partial(layer_kernel, n_wg, n_tp, (heads, slots,...]
where the time goes in v4:
time: 80.2 us; the launch traced here: 80.1 us
  Pallas kernels  79.4 us (99%)
    pallas_call x1, Pallas kernels, device_step(): pl.pallas_call(functools.partial(layer_kernel, n_wg, n_tp, (heads, slots,...  77.7 us
    pallas_call x1, Pallas kernels, device_step(): pl.pallas_call(functools.partial(write_kernel, PARTS), out_shape=tuple((j...  1.71 us

profile of v4, /device:TPU:97, one launch (start us, length us, event | category | flops | bytes accessed | tf_op | source)
XLA Modules:
  0.0 80.1 jit_solution(1735270667223395422)
XLA Ops:
  0.6 77.7 %decoder_layer.1 = (bf16[1024,1024]{1,0:T(8,128)(2,1)S(1)}, bf16[256,1024]{1,0:T(8,128)(2,1)S(1)}, bf16[256,1024]{1,0:T(8,128)(2,1)S(1)}) custom-call(bf16[1024,1024]{1,0:T(8,128)(2,1)} %tok_hbm.1, f32[1,128]{1,0:T(1,128)} %bitcast.24, f32[1,128]{1,0:T(1,128)} %bitcast.25, bf16[768,128]{1,0:T(8,128)(2,1)} %bitcast.20, bf16[256,128]{1,0:T(8,128)(2,1)} %bitcast.21, ...), custom_call_target="tpu_custom_call" | custom-call | tf_op jit(solution)/shard_map/decoder_layer/pallas_call | solution.py:547
  78.4 1.7 %write_results.1 = (bf16[1024,1024]{1,0:T(8,128)(2,1)}, bf16[256,1024]{1,0:T(8,128)(2,1)}, bf16[256,1024]{1,0:T(8,128)(2,1)}) custom-call(bf16[1024,1024]{1,0:T(8,128)(2,1)S(1)} %get-tuple-element.9.refs_0_, bf16[256,1024]{1,0:T(8,128)(2,1)S(1)} %get-tuple-element.10.refs_1_, bf16[256,1024]{1,0:T(8,128)(2,1)S(1)} %get-tuple-element.11.refs_2_), custom_call_target="tpu_custom_call" | custom-call | tf_op jit(solution)/shard_map/write_results/pallas_call | solution.py:582
